TPU v7x, 32 devices: a whole 2x2x4 slice. The times are simulated.
32 devices in a mesh: dp: 4 (over y, x), tensor: 8 (over z, core).
Axes of the slice: x: 2, y: 2, z: 4, core: 2. Of those that a mesh axis runs over, the one named last changes fastest.
Arguments:
- new_weight: float32 [5376, 8192], P(('dp', 'tensor')), may hold values from -0.0625 to 0.0625
- synced_weight: float32 [5376, 8192], P(('dp', 'tensor')), may hold values from -0.0625 to 0.0625
- resident: bfloat16 [5376, 8192], P(None, 'tensor'), may hold values from -0.0625 to 0.0625
- gain: float32 [5376], replicated, may hold values from 0.5 to 1.5
- query: bfloat16 [32, 2, 8192], P(('dp', 'tensor')), may hold values from -256 to 256
- cache_keys: bfloat16 [32, 768, 1024], P(('dp', 'tensor')), may hold values from -8 to 8
- cache_values: bfloat16 [32, 768, 1024], P(('dp', 'tensor')), may hold values from -6 to 6
- new_keys: bfloat16 [32, 2, 1024], P(('dp', 'tensor')), may hold values from -6 to 6
- new_values: bfloat16 [32, 2, 1024], P(('dp', 'tensor')), may hold values from -6 to 6
- cache_lengths: int32 [32], P(('dp', 'tensor')), may hold values from 2 to 768, as said below
Outputs:
- normed: bfloat16 [32, 2, 5376], P(('dp', 'tensor'))
Inputs may be any that keep to these rules, and one draw needn't show every extreme that they name: `cache_lengths`: some row has all 768 slots filled.
All inputs are finite; a program needn't handle non-finite values.
Results may differ from a plain program's by a relative error of at most 0.0069.
Values may be sent and summed in bfloat16 or wider, within the bound.
No kernel may reach another device: no remote copies, remote signals or barrier semaphores. Data moves between devices by JAX's collectives and lax.ppermute only.
A program may use at most 128 MiB of HBM per device.

v0:
```python
import jax
import jax.numpy as jnp
from jax import lax
from jax.sharding import PartitionSpec as P

HD = 128


def attend_block(query, cache_keys, cache_values, new_keys, new_values, cache_lengths):
    row_count = query.shape[0]
    step_count = query.shape[1]
    feature_count = query.shape[2]
    kv_features = cache_keys.shape[2]
    kv_heads = kv_features // HD
    grouping = feature_count // kv_features
    factor = HD ** (-0.5)
    grouped = query.reshape(row_count, step_count, kv_heads, grouping, HD)
    keys_old = cache_keys.reshape(row_count, -1, kv_heads, HD)
    values_old = cache_values.reshape(row_count, -1, kv_heads, HD)
    keys_new = new_keys.reshape(row_count, step_count, kv_heads, HD)
    values_new = new_values.reshape(row_count, step_count, kv_heads, HD)
    slot_count = keys_old.shape[1]
    past_scores = (
        jnp.einsum("rjkgd,rpkd->rjkgp", grouped, keys_old, preferred_element_type=jnp.float32)
        * factor
    )
    own_scores = (
        jnp.einsum("rjkgd,rikd->rjkgi", grouped, keys_new, preferred_element_type=jnp.float32)
        * factor
    )
    past_valid = jnp.arange(slot_count, dtype=jnp.int32)[None, :] < cache_lengths[:, None]
    positions = jnp.arange(step_count, dtype=jnp.int32)
    own_valid = positions[None, :] <= positions[:, None]
    past_scores = jnp.where(past_valid[:, None, None, None, :], past_scores, -jnp.inf)
    own_scores = jnp.where(own_valid[None, :, None, None, :], own_scores, -jnp.inf)
    highest = jnp.maximum(
        jnp.max(past_scores, axis=-1, keepdims=True), jnp.max(own_scores, axis=-1, keepdims=True)
    )
    past_exp = jnp.exp(past_scores - highest)
    own_exp = jnp.exp(own_scores - highest)
    total = jnp.sum(past_exp, axis=-1, keepdims=True) + jnp.sum(own_exp, axis=-1, keepdims=True)
    past_probs = (past_exp / total).astype(jnp.bfloat16)
    own_probs = (own_exp / total).astype(jnp.bfloat16)
    attended = jnp.einsum(
        "rjkgp,rpkd->rjkgd", past_probs, values_old, preferred_element_type=jnp.float32
    )
    attended = attended + jnp.einsum(
        "rjkgi,rikd->rjkgd", own_probs, values_new, preferred_element_type=jnp.float32
    )
    return attended.reshape(row_count, step_count, feature_count).astype(jnp.bfloat16)


def body(
    new_weight,
    synced_weight,
    resident,
    gain,
    query,
    cache_keys,
    cache_values,
    new_keys,
    new_values,
    cache_lengths,
):
    change = (new_weight - synced_weight).astype(jnp.bfloat16)
    sliced = lax.all_to_all(change, "tensor", split_axis=1, concat_axis=0, tiled=True)
    placed = lax.all_gather(sliced, "dp", axis=0, tiled=True)
    weight = (resident.astype(jnp.float32) + placed.astype(jnp.float32)).astype(jnp.bfloat16)
    attended = attend_block(query, cache_keys, cache_values, new_keys, new_values, cache_lengths)
    head_major = lax.all_to_all(attended, "tensor", split_axis=2, concat_axis=0, tiled=True)
    row_total = attended.shape[0] * lax.axis_size("tensor")
    flattened = head_major.reshape(row_total * head_major.shape[1], head_major.shape[2])
    product = lax.dot_general(
        flattened, weight, (((1,), (1,)), ((), ())), preferred_element_type=jnp.float32
    )
    projected = lax.psum_scatter(
        product.reshape(row_total, head_major.shape[1], weight.shape[0]),
        "tensor",
        scatter_dimension=0,
        tiled=True,
    )
    mean_square = jnp.mean(projected * projected, axis=-1, keepdims=True)
    return (projected * lax.rsqrt(mean_square + 1e-06) * gain).astype(jnp.bfloat16)


def solution(mesh):
    in_specs = (
        P(("dp", "tensor"), None),
        P(("dp", "tensor"), None),
        P(None, "tensor"),
        P(),
        P(("dp", "tensor"), None, None),
        P(("dp", "tensor"), None, None),
        P(("dp", "tensor"), None, None),
        P(("dp", "tensor"), None, None),
        P(("dp", "tensor"), None, None),
        P(("dp", "tensor")),
    )
    out_specs = P(("dp", "tensor"), None, None)
    return jax.shard_map(body, mesh=mesh, in_specs=in_specs, out_specs=out_specs, check_vma=False)
```

profile of v0, /device:TPU:0, one launch (start us, length us, event | category | flops | bytes accessed | tf_op | source)
XLA Modules:
  0.0 263.5 jit_solution(7980287687990632465)
XLA Ops:
  6.5 0.0 copy-start
  6.5 0.0 all-gather.2.cloned.1.call-start
  6.5 4.8 %subtract_convert_fusion = bf16[168,8192]{1,0:T(8,128)(2,1)S(1)} fusion(f32[168,8192]{1,0:T(8,128)} %param.10, f32[168,8192]{1,0:T(8,128)} %param.11), kind=kLoop, calls=%fused_computation.3 | loop fusion | flops 2752512 | bytes 13762560 | tf_op jit(solution)/shard_map/convert_element_type | solution.py:65
  11.3 0.3 copy.90
  11.6 0.0 copy-start.1
  11.6 69.5 %all_to_all.34 = bf16[168,8,1024]{2,0,1:T(8,128)(2,1)} all-to-all(bf16[168,8,1024]{2,0,1:T(8,128)(2,1)S(1)} %bitcast.92), channel_id=1, replica_groups=mesh['dp'=4,'tensor'=8] {'tensor'}, dimensions={1} | all-to-all | bytes 5505024 | tf_op jit(solution)/shard_map/all_to_all | solution.py:66
  81.1 0.0 all-gather.2.cloned.1.call-update
  81.1 0.0 all-reduce.3.cloned.1.call-start
  81.2 0.0 copy-done.1
  81.2 0.4 copy.48
  82.3 0.2 copy-done.2
  82.5 0.4 copy.50
  83.0 0.3 fusion.43
  83.3 0.6 fusion.42
  84.0 0.2 fusion.30
  84.2 0.2 fusion.37
  84.4 0.4 fusion.25
  84.9 6.8 %copy.35 = bf16[1,2,8192]{1,0,2:T(2,128)(2,1)} copy(bf16[1,2,8192]{2,1,0:T(2,128)(2,1)S(1)} %convert_element_type.50) | data formatting | bytes 65536 | tf_op jit(solution)/shard_map/convert_element_type | solution.py:50
  91.7 0.5 broadcast.53
  92.2 45.2 %reduce.5 = bf16[8192,2]{1,0:T(8,128)(2,1)S(1)} reduce(bf16[8192,1,2]{2,1,0:T(2,128)(2,1)} %bitcast.89, bf16[]{:T(256)} %broadcast.53), dimensions={1}, to_apply=%bitcast.79.reduce_sub_computation | reduce | bytes 65538
  137.4 3.3 %reshape.151 = bf16[8,2,1024]{2,1,0:T(2,128)(2,1)S(1)} reshape(bf16[8192,2]{1,0:T(8,128)(2,1)S(1)} %reduce.5) | data formatting | bytes 65536
  140.7 8.1 %all_to_all.35 = bf16[8,2,1024]{2,1,0:T(2,128)(2,1)S(1)} all-to-all(bf16[8,2,1024]{2,1,0:T(2,128)(2,1)S(1)} %reshape.151), channel_id=1, replica_groups=mesh['dp'=4,'tensor'=8] {'tensor'}, dimensions={0} | all-to-all | bytes 65536 | tf_op jit(solution)/shard_map/all_to_all | solution.py:70
  148.9 6.3 %reshape.152 = bf16[8192,1,2]{2,1,0:T(2,128)(2,1)} reshape(bf16[8,2,1024]{2,1,0:T(2,128)(2,1)S(1)} %all_to_all.35) | data formatting | bytes 65536
  155.2 8.1 %copy.36 = bf16[1,2,8192]{2,1,0:T(2,128)(2,1)S(1)} copy(bf16[1,2,8192]{1,0,2:T(2,128)(2,1)} %bitcast.90) | data formatting | bytes 65536 | tf_op jit(solution)/shard_map/all_to_all | solution.py:70
  163.3 26.2 %all-gather.2.cloned.1.call-done = bf16[5376,1024]{1,0:T(8,128)(2,1)} async-done(((bf16[1344,1024]{1,0:T(8,128)(2,1)}), bf16[5376,1024]{1,0:T(8,128)(2,1)}) %all-gather.2.cloned.1.call-update) | async-done | bytes 11010064 | tf_op jit(solution)/shard_map/all_gather | solution.py:67
  189.5 8.9 %fusion.1 = f32[8,2,5376]{2,0,1:T(8,128)S(1)} fusion(bf16[5376,1024]{1,0:T(8,128)(2,1)} %all-gather.2.cloned.1.call-done, bf16[5376,1024]{1,0:T(8,128)(2,1)} %param.12, bf16[1,2,8,1024]{3,1,2,0:T(2,128)(2,1)S(1)} %bitcast.98), kind=kOutput, calls=%fused_computation.2 | convolution fusion | flops 198180864 | bytes 22396928 | tf_op jit(solution)/shard_map/dot_general | solution.py:73
  198.4 0.9 copy.38
  199.3 0.0 all-reduce.3.cloned.1.call-update
  199.4 0.6 dynamic-slice
  200.0 53.0 %all-reduce.3.cloned.1.call-done = f32[8,2,5376]{2,1,0:T(2,128)} async-done(((f32[8,2,5376]{2,1,0:T(2,128)}), f32[8,2,5376]{2,1,0:T(2,128)}) %all-reduce.3.cloned.1.call-update) | async-done | bytes 344080
  252.9 1.6 multiply_reduce_fusion
  254.5 2.1 multiply_convert_fusion
  (18 shorter events, 0.1 us)
Async XLA Ops:
  6.5 77.7 %copy-start = (bf16[1,2,1024]{2,1,0:T(2,128)(2,1)S(1)}, bf16[1,2,1024]{2,1,0:T(2,128)(2,1)}, u32[]{:S(2)}) copy-start(bf16[1,2,1024]{2,1,0:T(2,128)(2,1)} %param.18) | copy-start | bytes 12292
  6.5 183.0 %all-gather.2.cloned.1.call-start = ((), (), s32[]{:S(2)}) async-start(), calls=%async_computation.2 | async-start | bytes 13762560 | tf_op jit(solution)/shard_map/all_gather | solution.py:67
  11.6 69.6 %copy-start.1 = (bf16[1,768,1024]{2,1,0:T(8,128)(2,1)S(1)}, bf16[1,768,1024]{2,1,0:T(8,128)(2,1)}, u32[]{:S(2)}) copy-start(bf16[1,768,1024]{2,1,0:T(8,128)(2,1)} %param.15) | copy-start | bytes 4718596
  81.1 1.4 copy-start.2
  81.1 1.9 copy-start.4
  81.1 1.9 copy-start.5
  81.1 171.8 %all-reduce.3.cloned.1.call-start = ((), (), s32[]{:S(2)}) async-start(), calls=%async_computation.3 | async-start | bytes 688128
  189.5 9.8 %copy-start.6 = (u32[32]{0:T(128)S(1)}, u32[32]{0:T(128)}, u32[]{:S(2)}) copy-start(u32[32]{0:T(128)} %constant.22) | copy-start | bytes 388
  189.5 65.0 %copy-start.3 = (f32[5376]{0:T(1024)S(1)}, f32[5376]{0:T(1024)}, u32[]{:S(2)}) copy-start(f32[5376]{0:T(1024)} %param.13) | copy-start | bytes 64516
Sparse Core Ops, SparseCore 0:
  81.2 108.2 all-gather.1
  199.5 53.4 all-reduce.2
where the time goes:
time: 264 us; the launch traced here: 263 us
  waiting for transfers between devices  79.2 us (30%)
  blocking collectives  77.6 us (29%)
  other arithmetic  54 us (20%)
  local copies, waits for them, and re-layouts  27.9 us (11%)
  between operations  14.2 us (5%)
  matrix products  10.4 us (4%)
    all_to_all x1, blocking collectives, body(): lax.all_to_all(change, 'tensor', split_axis=1, concat_axis=0, tiled=True)  69.5 us
    unnamed x3, waiting for transfers between devices  53 us
    unnamed x1, other arithmetic  45.2 us
    all_gather x1, waiting for transfers between devices, body(): placed = lax.all_gather(sliced, 'dp', axis=0, tiled=True)  26.2 us
    unnamed x20, local copies, waits for them, and re-layouts  11.9 us
    dot_general x1, matrix products, body(): lax.dot_general(flattened, weight, (((1,), (1,)), ((), ())), preferred_el...  8.88 us
    all_to_all x1, blocking collectives, body(): lax.all_to_all(attended, 'tensor', split_axis=2, concat_axis=0, tiled=True)  8.15 us
    all_to_all x1, local copies, waits for them, and re-layouts, body(): lax.all_to_all(attended, 'tensor', split_axis=2, concat_axis=0, tiled=True)  8.07 us
  transfers between devices with their start and end apart: 2, of which 2 were waited for; matrix products, arithmetic and copies ran while one was open for 28% of the time, Pallas kernels for 0%

commit v1 on v0

v1 whole, which is shorter than its diff:
```python
import functools

import jax
import jax.numpy as jnp
from jax import lax
from jax.experimental import pallas as pl
from jax.experimental.pallas import tpu as pltpu
from jax.sharding import PartitionSpec as P

HD = 128
CORES = 2
MOST = 32
FEW = 4
NT = (((1,), (1,)), ((), ()))
NN = (((1,), (0,)), ((), ()))


def dot(a, b, dims):
    return lax.dot_general(a, b, dims, preferred_element_type=jnp.float32)


def divisor(total, most, unit):
    fits = [n for n in range(unit, min(total, most) + 1, unit) if total % n == 0]
    return fits[-1] if fits else total


def attend_kernel(length_ref, query_ref, keys_ref, values_ref, new_keys_ref, new_values_ref, out_ref, *, grouping):
    steps, width = new_keys_ref.shape[1], new_keys_ref.shape[2]
    heads = width // HD
    slots = keys_ref.shape[1]
    factor = HD ** (-0.5)
    query = query_ref[0].astype(jnp.float32)
    block_rows = grouping * steps
    rows = heads * block_rows
    bands = []
    for k in range(heads):
        pieces = [query[:, (k * grouping + g) * HD : (k * grouping + g + 1) * HD] for g in range(grouping)]
        own = jnp.concatenate(pieces, axis=0)
        line = [own if i == k else jnp.zeros_like(own) for i in range(heads)]
        bands.append(jnp.concatenate(line, axis=1))
    stacked = jnp.concatenate(bands, axis=0).astype(jnp.bfloat16)

    padding = jnp.zeros((8 - steps % 8, width), jnp.float32)
    keys_new = jnp.concatenate([new_keys_ref[0].astype(jnp.float32), padding], axis=0).astype(jnp.bfloat16)
    values_new = jnp.concatenate([new_values_ref[0].astype(jnp.float32), padding], axis=0).astype(jnp.bfloat16)

    past = dot(stacked, keys_ref[0], NT) * factor
    own = dot(stacked, keys_new, NT) * factor
    slot = lax.broadcasted_iota(jnp.int32, past.shape, 1)
    past = jnp.where(slot < length_ref[pl.program_id(0)], past, -jnp.inf)
    column = lax.broadcasted_iota(jnp.int32, own.shape, 1)
    position = lax.rem(lax.broadcasted_iota(jnp.int32, own.shape, 0), steps)
    own = jnp.where(column <= position, own, -jnp.inf)
    highest = jnp.maximum(jnp.max(past, axis=1, keepdims=True), jnp.max(own, axis=1, keepdims=True))
    past = jnp.exp(past - highest)
    own = jnp.exp(own - highest)
    total = jnp.sum(past, axis=1, keepdims=True) + jnp.sum(own, axis=1, keepdims=True)
    past = (past / total).astype(jnp.bfloat16)
    own = (own / total).astype(jnp.bfloat16)
    attended = dot(past, values_ref[0], NN) + dot(own, values_new, NN)
    for k in range(heads):
        for g in range(grouping):
            at = k * block_rows + g * steps
            head = k * grouping + g
            out_ref[0, :, head * HD : (head + 1) * HD] = attended[at : at + steps, k * HD : (k + 1) * HD].astype(
                jnp.bfloat16
            )


def attend(query, cache_keys, cache_values, new_keys, new_values, cache_lengths):
    rows, steps, features = query.shape
    slots, kv_features = cache_keys.shape[1:]
    grouping = features // kv_features
    width = HD * 2 if kv_features % (HD * 2) == 0 else HD
    wide = lambda r, h, *_: (r, 0, h)
    return pl.pallas_call(
        functools.partial(attend_kernel, grouping=grouping),
        out_shape=jax.ShapeDtypeStruct(query.shape, jnp.bfloat16),
        grid_spec=pltpu.PrefetchScalarGridSpec(
            num_scalar_prefetch=1,
            grid=(rows, kv_features // width),
            in_specs=[
                pl.BlockSpec((1, steps, width * grouping), wide),
                pl.BlockSpec((1, slots, width), wide),
                pl.BlockSpec((1, slots, width), wide),
                pl.BlockSpec((1, steps, width), wide),
                pl.BlockSpec((1, steps, width), wide),
            ],
            out_specs=pl.BlockSpec((1, steps, width * grouping), wide),
        ),
        name="attend",
    )(cache_lengths, query, cache_keys, cache_values, new_keys, new_values)


def weights_kernel(group_ref, new_ref, synced_ref, resident_ref, out_ref):
    blocks, depth = out_ref.shape[1], out_ref.shape[3]
    for b in range(blocks):
        at = slice(b * depth, (b + 1) * depth)
        out_ref[0, b] = (new_ref[:, at] - synced_ref[:, at]).astype(jnp.bfloat16)
    out_ref[1] = resident_ref[...]


def local_weights(new_weight, synced_weight, resident, group, groups):
    rows, features = new_weight.shape
    depth = resident.shape[1]
    blocks = features // depth
    stored = resident.reshape(groups * blocks, rows, depth)
    take = divisor(rows, 24, 8)
    return pl.pallas_call(
        weights_kernel,
        out_shape=jax.ShapeDtypeStruct((2, blocks, rows, depth), jnp.bfloat16),
        grid_spec=pltpu.PrefetchScalarGridSpec(
            num_scalar_prefetch=1,
            grid=(rows // take,),
            in_specs=[
                pl.BlockSpec((take, features), lambda i, g: (i, 0)),
                pl.BlockSpec((take, features), lambda i, g: (i, 0)),
                pl.BlockSpec((blocks, take, depth), lambda i, g: (g[0], i, 0)),
            ],
            out_specs=pl.BlockSpec((2, blocks, take, depth), lambda i, g: (0, 0, i, 0)),
        ),
        name="local_weights",
    )(group, new_weight, synced_weight, stored)


def project_kernel(place_ref, *refs, parts):
    gathered, (own_ref, other_ref, out_ref, rows_ref, sums_ref) = refs[:parts], refs[parts:]
    owners, steps, columns = out_ref.shape
    blocks, width, depth = own_ref.shape[1:]
    first = pl.program_id(0) * owners
    pieces = []
    for part in gathered:
        for k in range(part.shape[0]):
            pieces.append(part[k].astype(jnp.float32))
    rows_ref[...] = jnp.concatenate(pieces, axis=0).astype(jnp.bfloat16)
    for source, ref in enumerate((own_ref, other_ref)):
        block = place_ref[source]
        rows = rows_ref[:, pl.ds(pl.multiple_of(block * depth, depth), depth)]
        for b in range(blocks):
            value = dot(rows, ref[1, b], NT)
            if source == 0:
                sums_ref[b] = value
            else:
                sums_ref[b] += value
    for source, ref in enumerate((own_ref, other_ref)):
        value = dot(rows_ref[:, :depth], ref[0, 0], NT)
        for b in range(1, blocks):
            value += dot(rows_ref[:, b * depth : (b + 1) * depth], ref[0, b], NT)
        sums_ref[place_ref[source]] += value
    for k in range(owners):
        owner = place_ref[2 + first + k] - first
        at = slice(k * steps, (k + 1) * steps)
        for b in range(blocks):
            out_ref[owner, :, b * width : (b + 1) * width] = sums_ref[b, at, :]


def project(gathered, own, other, place, owners, steps):
    blocks, width, depth = own.shape[1:]
    take = owners if len(gathered) > 1 else divisor(owners, MOST, 1)
    several = owners > take
    whole = pl.BlockSpec(memory_space=pltpu.VMEM)
    cut = lambda s: pl.BlockSpec((take, *s[1:]), lambda i: (i, 0, 0)) if several else whole
    out = jax.ShapeDtypeStruct((owners, steps, blocks * width), jnp.float32)
    return pl.pallas_call(
        functools.partial(project_kernel, parts=len(gathered)),
        out_shape=out,
        grid=(owners // take,),
        in_specs=[pl.BlockSpec(memory_space=pltpu.SMEM), *[cut(g.shape) for g in gathered], whole, whole],
        out_specs=cut(out.shape),
        scratch_shapes=[
            pltpu.VMEM((take * steps, blocks * depth), jnp.bfloat16),
            pltpu.VMEM((blocks, take * steps, width), jnp.float32),
        ],
        name="project",
    )(place, *gathered, own, other)


def norm_kernel(partial_ref, gain_ref, out_ref, sums_ref, *, groups):
    owners, steps, columns = partial_ref.shape
    chips = owners // groups
    for d in range(groups):
        value = partial_ref[d * chips]
        for z in range(1, chips):
            value += partial_ref[d * chips + z]
        sums_ref[:, d * columns : (d + 1) * columns] = value
    projected = sums_ref[...]
    mean_square = jnp.mean(projected * projected, axis=1, keepdims=True)
    out_ref[0] = (projected * lax.rsqrt(mean_square + 1e-06) * gain_ref[...]).astype(jnp.bfloat16)


def normalise(partial, gain, groups):
    steps, columns = partial.shape[1], partial.shape[2] * groups
    return pl.pallas_call(
        functools.partial(norm_kernel, groups=groups),
        out_shape=jax.ShapeDtypeStruct((1, steps, columns), jnp.bfloat16),
        in_specs=[pl.BlockSpec(memory_space=pltpu.VMEM)] * 2,
        out_specs=pl.BlockSpec(memory_space=pltpu.VMEM),
        scratch_shapes=[pltpu.VMEM((steps, columns), jnp.float32)],
        name="normalise",
    )(partial, gain.reshape(1, columns))


def body(
    new_weight,
    synced_weight,
    resident,
    gain,
    query,
    cache_keys,
    cache_values,
    new_keys,
    new_values,
    cache_lengths,
):
    groups, devices = lax.axis_size("dp"), lax.axis_size("tensor")
    chips = devices // CORES
    group, device = lax.axis_index("dp"), lax.axis_index("tensor")
    chip = device // CORES
    count, steps, features = query.shape

    def exchange(value, axis, size, unit, hop):
        return lax.ppermute(value, axis, [(i, (i // unit ^ hop) * unit + i % unit) for i in range(size)])

    attended = attend(query, cache_keys, cache_values, new_keys, new_values, cache_lengths)
    if chips <= FEW and chips & (chips - 1) == 0:
        column = jnp.concatenate(
            [attended] + [exchange(attended, "tensor", devices, CORES, hop) for hop in range(1, chips)], axis=0
        )
        chip_order = [chip ^ hop for hop in range(chips)]
    else:
        alike = [[i * CORES + c for i in range(chips)] for c in range(CORES)]
        column = lax.all_gather(attended, "tensor", axis=0, tiled=True, axis_index_groups=alike)
        chip_order = list(range(chips))
    if groups <= FEW and groups & (groups - 1) == 0:
        gathered = [column] + [exchange(column, "dp", groups, 1, hop) for hop in range(1, groups)]
        group_order = [group ^ hop for hop in range(groups)]
    else:
        gathered = [lax.all_gather(column, "dp", axis=0, tiled=True)]
        group_order = list(range(groups))

    own = local_weights(new_weight, synced_weight, resident, group.reshape(1), groups)
    other = exchange(own, "tensor", devices, 1, 1)
    owners = jnp.stack(
        [device, device ^ 1]
        + [(g * chips + c) * count + r for g in group_order for c in chip_order for r in range(count)]
    ).astype(jnp.int32)
    partial = project(gathered, own, other, owners, groups * chips * count, steps)
    alike = [
        [g * devices + i * CORES + c for g in range(groups) for i in range(chips)] for c in range(CORES)
    ]
    summed = lax.all_to_all(
        partial, ("dp", "tensor"), split_axis=0, concat_axis=0, tiled=True, axis_index_groups=alike
    )
    return normalise(summed, gain, groups)


def solution(mesh):
    in_specs = (
        P(("dp", "tensor"), None),
        P(("dp", "tensor"), None),
        P(None, "tensor"),
        P(),
        P(("dp", "tensor"), None, None),
        P(("dp", "tensor"), None, None),
        P(("dp", "tensor"), None, None),
        P(("dp", "tensor"), None, None),
        P(("dp", "tensor"), None, None),
        P(("dp", "tensor")),
    )
    out_specs = P(("dp", "tensor"), None, None)
    return jax.shard_map(body, mesh=mesh, in_specs=in_specs, out_specs=out_specs, check_vma=False)
```

time: 264 us -> 60.8 us (0.23)
  blocking collectives: 77.6 us -> 0 us
  waiting for transfers between devices: 79.2 us -> 18 us
  other arithmetic: 54 us -> 0.99 us
  Pallas kernels: 0 us -> 25.3 us
  local copies, waits for them, and re-layouts: 27.9 us -> 2.6 us
  between operations: 14.2 us -> 0.71 us
  starting transfers between devices: 0.04 us -> 12.7 us
  matrix products: 10.4 us -> 0 us
    all_to_all x2 -> x0, blocking collectives: 77.6 us -> none  [the longest x1 69.5 us: body(): lax.all_to_all(change, 'tensor', split_axis=1, concat_axis=0, tiled=True)]
    unnamed x3 -> x0, waiting for transfers between devices: 53 us -> none
    unnamed x1 -> x0, other arithmetic: 45.2 us -> none
    all_gather x1 -> x0, waiting for transfers between devices: 26.2 us -> none  [body(): placed = lax.all_gather(sliced, 'dp', axis=0, tiled=True)]
    pallas_call x0 -> x4, Pallas kernels: none -> 25.3 us  [the longest x1 9.34 us: project(): pl.pallas_call(functools.partial(project_kernel, parts=len(gathered)), ou...]
    ppermute x0 -> x7, waiting for transfers between devices: none -> 10.9 us  [exchange(): lax.ppermute(value, axis, [(i, (i // unit ^ hop) * unit + i % unit) for i...]
    unnamed x20 -> x12, local copies, waits for them, and re-layouts: 11.9 us -> 1.34 us
    dot_general x5 -> x0, matrix products: 10.4 us -> none  [the longest x1 8.88 us: body(): lax.dot_general(flattened, weight, (((1,), (1,)), ((), ())), preferred_el...]
  transfers between devices with their start and end apart: 2 -> 8, of which waited for: 2 -> 5; matrix products, arithmetic and copies ran while one was open for 28% -> 4% of each run, Pallas kernels for 0% -> 8%
where the time goes in v1:
time: 60.8 us; the launch traced here: 60.4 us
  Pallas kernels  25.3 us (42%)
  waiting for transfers between devices  18 us (30%)
  starting transfers between devices  12.7 us (21%)
  local copies, waits for them, and re-layouts  2.6 us (4%)
  other arithmetic  0.99 us (2%)
  between operations  0.71 us (1%)
    ppermute x7, waiting for transfers between devices, exchange(): lax.ppermute(value, axis, [(i, (i // unit ^ hop) * unit + i % unit) for i...  10.9 us
    pallas_call x1, Pallas kernels, project(): pl.pallas_call(functools.partial(project_kernel, parts=len(gathered)), ou...  9.34 us
    pallas_call x1, Pallas kernels, local_weights(): pl.pallas_call(weights_kernel, out_shape=jax.ShapeDtypeStruct((2, blocks,...  9.24 us
    ppermute x7, starting transfers between devices, exchange(): lax.ppermute(value, axis, [(i, (i // unit ^ hop) * unit + i % unit) for i...  9.2 us
    all_to_all x1, waiting for transfers between devices, body(): lax.all_to_all(partial, ('dp', 'tensor'), split_axis=0, concat_axis=0, ti...  7.15 us
    pallas_call x1, Pallas kernels, attend(): pl.pallas_call(functools.partial(attend_kernel, grouping=grouping), out_s...  4.96 us
    all_to_all x1, starting transfers between devices, body(): lax.all_to_all(partial, ('dp', 'tensor'), split_axis=0, concat_axis=0, ti...  3.52 us
    pallas_call x1, Pallas kernels, normalise(): pl.pallas_call(functools.partial(norm_kernel, groups=groups), out_shape=j...  1.75 us
  transfers between devices with their start and end apart: 8, of which 5 were waited for; matrix products, arithmetic and copies ran while one was open for 4% of the time, Pallas kernels for 8%

profile of v1, /device:TPU:0, one launch (start us, length us, event | category | flops | bytes accessed | tf_op | source)
XLA Modules:
  0.0 60.4 jit_solution(7391303763718362393)
XLA Ops:
  0.0 9.2 %local_weights.1.refs_4_ = bf16[2,8,168,1024]{3,2,1,0:T(8,128)(2,1)} custom-call(s32[1]{0:T(128)} %bitcast.18.group_ref, f32[168,8192]{1,0:T(8,128)} %new_ref.1, f32[168,8192]{1,0:T(8,128)} %synced_ref.1, bf16[32,168,1024]{2,1,0:T(8,128)(2,1)} %bitcast.20), custom_call_target="tpu_custom_call" | custom-call | tf_op jit(solution)/shard_map/local_weights/pallas_call | solution.py:109
  9.2 0.5 collective-permute-start.6
  10.4 5.0 %attend.1 = bf16[1,2,8192]{2,1,0:T(2,128)(2,1)} custom-call(s32[1]{0:T(128)S(6)} %copy.11.length_ref, bf16[1,2,8192]{2,1,0:T(2,128)(2,1)} %query_ref.1, bf16[1,768,1024]{2,1,0:T(8,128)(2,1)} %keys_ref.1, bf16[1,768,1024]{2,1,0:T(8,128)(2,1)} %values_ref.1, bf16[1,2,1024]{2,1,0:T(2,128)(2,1)} %new_keys_ref.1, bf16[1,2,1024]{2,1,0:T(2,128)(2,1)} %new_values_ref.1), custom_call_target="tpu_custom_call" | custom-call | tf_op jit(solution)/shard_map/attend/pallas_call | solution.py:76
  15.3 2.6 %collective-permute-start = (bf16[1,2,8192]{2,1,0:T(2,128)(2,1)}, bf16[1,2,8192]{2,1,0:T(2,128)(2,1)S(1)}, u32[]{:S(2)}, u32[]{:S(2)}) collective-permute-start(bf16[1,2,8192]{2,1,0:T(2,128)(2,1)} %attend.1), channel_id=1, source_target_pairs={{0,2},{1,3},{2,0},{3,1},{4,6},{5,7},{6,4},{7,5},{8,10},{9,11},{10,... | collective-permute-start | bytes 98312 | tf_op jit(solution)/shard_map/ppermute | solution.py:222
  17.9 2.6 %collective-permute-start.1 = (bf16[1,2,8192]{2,1,0:T(2,128)(2,1)}, bf16[1,2,8192]{2,1,0:T(2,128)(2,1)S(1)}, u32[]{:S(2)}, u32[]{:S(2)}) collective-permute-start(bf16[1,2,8192]{2,1,0:T(2,128)(2,1)} %attend.1), channel_id=1, source_target_pairs={{0,4},{1,5},{2,6},{3,7},{4,0},{5,1},{6,2},{7,3},{8,12},{9,13},{10,... | collective-permute-start | bytes 98312 | tf_op jit(solution)/shard_map/ppermute | solution.py:222
  20.5 0.0 collective-permute-start.2
  20.5 0.0 collective-permute-done
  20.5 3.0 %collective-permute-done.1 = bf16[1,2,8192]{2,1,0:T(2,128)(2,1)S(1)} collective-permute-done((bf16[1,2,8192]{2,1,0:T(2,128)(2,1)}, bf16[1,2,8192]{2,1,0:T(2,128)(2,1)S(1)}, u32[]{:S(2)}, u32[]{:S(2)}) %collective-permute-start.1) | collective-permute-done | bytes 32800 | tf_op jit(solution)/shard_map/ppermute | solution.py:222
  23.5 3.0 %collective-permute-done.2 = bf16[1,2,8192]{2,1,0:T(2,128)(2,1)S(1)} collective-permute-done((bf16[1,2,8192]{2,1,0:T(2,128)(2,1)}, bf16[1,2,8192]{2,1,0:T(2,128)(2,1)S(1)}, u32[]{:S(2)}, u32[]{:S(2)}) %collective-permute-start.2) | collective-permute-done | bytes 32800 | tf_op jit(solution)/shard_map/ppermute | solution.py:222
  26.4 1.0 %pad_maximum_fusion.refs_0_ = bf16[4,2,8192]{2,1,0:T(2,128)(2,1)S(1)} fusion(bf16[1,2,8192]{2,1,0:T(2,128)(2,1)S(1)} %collective-permute-done.2, bf16[1,2,8192]{2,1,0:T(2,128)(2,1)S(1)} %collective-permute-done.1, bf16[1,2,8192]{2,1,0:T(2,128)(2,1)S(1)} %collective-permute-done, bf16[1,2,8192]{2,1,0:T(2,128)(2,1)} %attend.1), kind=kLoop, calls=%fused_computation | loop fusion | flops 196608 | bytes 262144 | tf_op jit(solution)/shard_map/concatenate | solution.py:226
  27.4 0.0 copy-start.1
  27.4 1.6 %collective-permute-start.3 = (bf16[4,2,8192]{2,1,0:T(2,128)(2,1)S(1)}, bf16[4,2,8192]{2,1,0:T(2,128)(2,1)S(1)}, u32[]{:S(2)}, u32[]{:S(2)}) collective-permute-start(bf16[4,2,8192]{2,1,0:T(2,128)(2,1)S(1)} %pad_maximum_fusion.refs_0_), channel_id=1, source_target_pairs={{0,8},{8,0},{16,24},{24,16},{1,9},{9,1},{17,25},{25,17},{2,10},{10... | collective-permute-start | bytes 393224 | tf_op jit(solution)/shard_map/ppermute | solution.py:222
  29.0 1.5 %collective-permute-start.4 = (bf16[4,2,8192]{2,1,0:T(2,128)(2,1)S(1)}, bf16[4,2,8192]{2,1,0:T(2,128)(2,1)S(1)}, u32[]{:S(2)}, u32[]{:S(2)}) collective-permute-start(bf16[4,2,8192]{2,1,0:T(2,128)(2,1)S(1)} %pad_maximum_fusion.refs_0_), channel_id=1, source_target_pairs={{0,16},{8,24},{16,0},{24,8},{1,17},{9,25},{17,1},{25,9},{2,18},{10... | collective-permute-start | bytes 393224 | tf_op jit(solution)/shard_map/ppermute | solution.py:222
  30.5 0.5 collective-permute-start.5
  31.0 0.6 %stack.75.place_ref = s32[18]{0:T(128)} concatenate(s32[1]{0:T(128)} %bitcast, s32[1]{0:T(128)} %bitcast.1, s32[1]{0:T(128)} %bitcast.2, s32[1]{0:T(128)} %bitcast.3, s32[1]{0:T(128)} %bitcast.4, s32[1]{0:T(128)} %bitcast.5, s32[1]{0:T(128)} %bitcast.6, s32[1]{0:T(128)} %bitcast.7, s32[1]{0:T(128)} %bitcast.8, s32[1]{0:T(128)} %bitcast.9, s32[1]{0:T(128)} %bitcast.10, ...), dimensions={0} | concatenate | bytes 144 | tf_op jit(solution)/shard_map/stack | solution.py:243
  31.6 0.0 copy-start.5
  31.6 2.0 %collective-permute-done.3.refs_1_ = bf16[4,2,8192]{2,1,0:T(2,128)(2,1)S(1)} collective-permute-done((bf16[4,2,8192]{2,1,0:T(2,128)(2,1)S(1)}, bf16[4,2,8192]{2,1,0:T(2,128)(2,1)S(1)}, u32[]{:S(2)}, u32[]{:S(2)}) %collective-permute-start.3) | collective-permute-done | bytes 131104 | tf_op jit(solution)/shard_map/ppermute | solution.py:222
  33.6 0.0 copy-start.2
  33.6 3.0 %collective-permute-done.4.refs_2_ = bf16[4,2,8192]{2,1,0:T(2,128)(2,1)S(1)} collective-permute-done((bf16[4,2,8192]{2,1,0:T(2,128)(2,1)S(1)}, bf16[4,2,8192]{2,1,0:T(2,128)(2,1)S(1)}, u32[]{:S(2)}, u32[]{:S(2)}) %collective-permute-start.4) | collective-permute-done | bytes 131104 | tf_op jit(solution)/shard_map/ppermute | solution.py:222
  36.6 0.0 collective-permute-done.5.refs_3_
  36.6 0.0 collective-permute-done.6.refs_5_
  36.6 0.0 copy-done.1
  36.6 0.0 copy-done.2
  36.6 0.6 %copy-done.3 = bf16[4,2,8192]{2,1,0:T(2,128)(2,1)} copy-done((bf16[4,2,8192]{2,1,0:T(2,128)(2,1)}, bf16[4,2,8192]{2,1,0:T(2,128)(2,1)S(1)}, u32[]{:S(2)}) %copy-start.3) | copy-done | bytes 131096
  37.3 0.0 copy-done.4
  37.3 9.3 %project.1 = f32[16,2,1344]{2,1,0:T(2,128)} custom-call(s32[18]{0:T(128)} %stack.75.place_ref, bf16[4,2,8192]{2,1,0:T(2,128)(2,1)} %copy-done.1, bf16[4,2,8192]{2,1,0:T(2,128)(2,1)} %copy-done.2, bf16[4,2,8192]{2,1,0:T(2,128)(2,1)} %copy-done.3, bf16[4,2,8192]{2,1,0:T(2,128)(2,1)} %copy-done.4, bf16[2,8,168,1024]{3,2,1,0:T(8,128)(2,1)} %local_weights.1.refs_4_, ...), custom_call_target="tpu_custom_call" | custom-call | tf_op jit(solution)/shard_map/project/pallas_call | solution.py:164
  46.6 3.5 %all-to-all-start = ((f32[16,2,1344]{2,1,0:T(2,128)}), f32[16,2,1344]{2,1,0:T(2,128)S(1)}, u32[]{:S(2)}, u32[]{:S(2)}) async-start(f32[16,2,1344]{2,1,0:T(2,128)} %project.1), calls=%async_computation | async-start | bytes 360448 | tf_op jit(solution)/shard_map/all_to_all | solution.py:251
  50.2 0.0 copy-done.5
  50.2 0.6 %reshape.11.gain_ref = f32[1,5376]{1,0:T(1,128)} reshape(f32[5376]{0:T(1024)S(1)} %copy-done.5) | data formatting | bytes 43008 | tf_op jit(solution)/shard_map/reshape | solution.py:200
  50.8 7.2 %all-to-all-done.partial_ref = f32[16,2,1344]{2,1,0:T(2,128)S(1)} async-done(((f32[16,2,1344]{2,1,0:T(2,128)}), f32[16,2,1344]{2,1,0:T(2,128)S(1)}, u32[]{:S(2)}, u32[]{:S(2)}) %all-to-all-start) | async-done | bytes 172064 | tf_op jit(solution)/shard_map/all_to_all | solution.py:251
  58.0 0.7 %copy-done = f32[16,2,1344]{2,1,0:T(2,128)} copy-done((f32[16,2,1344]{2,1,0:T(2,128)}, f32[16,2,1344]{2,1,0:T(2,128)S(1)}, u32[]{:S(2)}) %copy-start) | copy-done | bytes 172056
  58.6 1.8 %normalise.1 = bf16[1,2,5376]{2,1,0:T(2,128)(2,1)} custom-call(f32[16,2,1344]{2,1,0:T(2,128)} %copy-done, f32[1,5376]{1,0:T(1,128)} %reshape.11.gain_ref), custom_call_target="tpu_custom_call" | custom-call | tf_op jit(solution)/shard_map/normalise/pallas_call | solution.py:193
  (3 shorter events, 0.0 us)
Async XLA Ops:
  9.2 27.4 %collective-permute-start.6 = (bf16[2,8,168,1024]{3,2,1,0:T(8,128)(2,1)}, bf16[2,8,168,1024]{3,2,1,0:T(8,128)(2,1)}, u32[]{:S(2)}, u32[]{:S(2)}) collective-permute-start(bf16[2,8,168,1024]{3,2,1,0:T(8,128)(2,1)} %local_weights.1.refs_4_), channel_id=1, source_target_pairs={{0,1},{1,0},{2,3},{3,2},{4,5},{5,4},{6,7},{7,6},{8,9},{9,8},{10,11... | collective-permute-start | bytes 16515080 | tf_op jit(solution)/shard_map/ppermute | solution.py:222
  15.3 5.2 %collective-permute-start = (bf16[1,2,8192]{2,1,0:T(2,128)(2,1)}, bf16[1,2,8192]{2,1,0:T(2,128)(2,1)S(1)}, u32[]{:S(2)}, u32[]{:S(2)}) collective-permute-start(bf16[1,2,8192]{2,1,0:T(2,128)(2,1)} %attend.1), channel_id=1, source_target_pairs={{0,2},{1,3},{2,0},{3,1},{4,6},{5,7},{6,4},{7,5},{8,10},{9,11},{10,... | collective-permute-start | bytes 98312 | tf_op jit(solution)/shard_map/ppermute | solution.py:222
  17.9 5.5 %collective-permute-start.1 = (bf16[1,2,8192]{2,1,0:T(2,128)(2,1)}, bf16[1,2,8192]{2,1,0:T(2,128)(2,1)S(1)}, u32[]{:S(2)}, u32[]{:S(2)}) collective-permute-start(bf16[1,2,8192]{2,1,0:T(2,128)(2,1)} %attend.1), channel_id=1, source_target_pairs={{0,4},{1,5},{2,6},{3,7},{4,0},{5,1},{6,2},{7,3},{8,12},{9,13},{10,... | collective-permute-start | bytes 98312 | tf_op jit(solution)/shard_map/ppermute | solution.py:222
  20.5 5.9 %collective-permute-start.2 = (bf16[1,2,8192]{2,1,0:T(2,128)(2,1)}, bf16[1,2,8192]{2,1,0:T(2,128)(2,1)S(1)}, u32[]{:S(2)}, u32[]{:S(2)}) collective-permute-start(bf16[1,2,8192]{2,1,0:T(2,128)(2,1)} %attend.1), channel_id=1, source_target_pairs={{0,6},{1,7},{2,4},{3,5},{4,2},{5,3},{6,0},{7,1},{8,14},{9,15},{10,... | collective-permute-start | bytes 98312 | tf_op jit(solution)/shard_map/ppermute | solution.py:222
  27.4 9.2 %copy-start.1 = (bf16[4,2,8192]{2,1,0:T(2,128)(2,1)}, bf16[4,2,8192]{2,1,0:T(2,128)(2,1)S(1)}, u32[]{:S(2)}) copy-start(bf16[4,2,8192]{2,1,0:T(2,128)(2,1)S(1)} %pad_maximum_fusion.refs_0_) | copy-start | bytes 393220
  27.4 6.2 %collective-permute-start.3 = (bf16[4,2,8192]{2,1,0:T(2,128)(2,1)S(1)}, bf16[4,2,8192]{2,1,0:T(2,128)(2,1)S(1)}, u32[]{:S(2)}, u32[]{:S(2)}) collective-permute-start(bf16[4,2,8192]{2,1,0:T(2,128)(2,1)S(1)} %pad_maximum_fusion.refs_0_), channel_id=1, source_target_pairs={{0,8},{8,0},{16,24},{24,16},{1,9},{9,1},{17,25},{25,17},{2,10},{10... | collective-permute-start | bytes 393224 | tf_op jit(solution)/shard_map/ppermute | solution.py:222
  29.0 7.6 %collective-permute-start.4 = (bf16[4,2,8192]{2,1,0:T(2,128)(2,1)S(1)}, bf16[4,2,8192]{2,1,0:T(2,128)(2,1)S(1)}, u32[]{:S(2)}, u32[]{:S(2)}) collective-permute-start(bf16[4,2,8192]{2,1,0:T(2,128)(2,1)S(1)} %pad_maximum_fusion.refs_0_), channel_id=1, source_target_pairs={{0,16},{8,24},{16,0},{24,8},{1,17},{9,25},{17,1},{25,9},{2,18},{10... | collective-permute-start | bytes 393224 | tf_op jit(solution)/shard_map/ppermute | solution.py:222
  30.5 6.1 %collective-permute-start.5 = (bf16[4,2,8192]{2,1,0:T(2,128)(2,1)S(1)}, bf16[4,2,8192]{2,1,0:T(2,128)(2,1)S(1)}, u32[]{:S(2)}, u32[]{:S(2)}) collective-permute-start(bf16[4,2,8192]{2,1,0:T(2,128)(2,1)S(1)} %pad_maximum_fusion.refs_0_), channel_id=1, source_target_pairs={{0,24},{8,16},{16,8},{24,0},{1,25},{9,17},{17,9},{25,1},{2,26},{10... | collective-permute-start | bytes 393224 | tf_op jit(solution)/shard_map/ppermute | solution.py:222
  31.6 18.5 %copy-start.5 = (f32[5376]{0:T(1024)S(1)}, f32[5376]{0:T(1024)}, u32[]{:S(2)}) copy-start(f32[5376]{0:T(1024)} %param.13) | copy-start | bytes 64516
  33.6 3.0 %copy-start.2 = (bf16[4,2,8192]{2,1,0:T(2,128)(2,1)}, bf16[4,2,8192]{2,1,0:T(2,128)(2,1)S(1)}, u32[]{:S(2)}) copy-start(bf16[4,2,8192]{2,1,0:T(2,128)(2,1)S(1)} %collective-permute-done.3.refs_1_) | copy-start | bytes 393220
  36.6 0.6 %copy-start.3 = (bf16[4,2,8192]{2,1,0:T(2,128)(2,1)}, bf16[4,2,8192]{2,1,0:T(2,128)(2,1)S(1)}, u32[]{:S(2)}) copy-start(bf16[4,2,8192]{2,1,0:T(2,128)(2,1)S(1)} %collective-permute-done.4.refs_2_) | copy-start | bytes 393220
  36.6 0.7 %copy-start.4 = (bf16[4,2,8192]{2,1,0:T(2,128)(2,1)}, bf16[4,2,8192]{2,1,0:T(2,128)(2,1)S(1)}, u32[]{:S(2)}) copy-start(bf16[4,2,8192]{2,1,0:T(2,128)(2,1)S(1)} %collective-permute-done.5.refs_3_) | copy-start | bytes 393220
  46.6 11.3 %all-to-all-start = ((f32[16,2,1344]{2,1,0:T(2,128)}), f32[16,2,1344]{2,1,0:T(2,128)S(1)}, u32[]{:S(2)}, u32[]{:S(2)}) async-start(f32[16,2,1344]{2,1,0:T(2,128)} %project.1), calls=%async_computation | async-start | bytes 360448 | tf_op jit(solution)/shard_map/all_to_all | solution.py:251
  57.9 0.7 %copy-start = (f32[16,2,1344]{2,1,0:T(2,128)}, f32[16,2,1344]{2,1,0:T(2,128)S(1)}, u32[]{:S(2)}) copy-start(f32[16,2,1344]{2,1,0:T(2,128)S(1)} %all-to-all-done.partial_ref) | copy-start | bytes 516100

commit v2 on v1

v2 whole, which is shorter than its diff:
```python
import functools

import jax
import jax.numpy as jnp
from jax import lax
from jax.experimental import pallas as pl
from jax.experimental.pallas import tpu as pltpu
from jax.sharding import PartitionSpec as P


HD = 128
CORES = 2
MOST = 32
FEW = 4
NT = (((1,), (1,)), ((), ()))
NN = (((1,), (0,)), ((), ()))


def dot(a, b, dims):
    return lax.dot_general(a, b, dims, preferred_element_type=jnp.float32)


def limit(mebibytes):
    return pltpu.CompilerParams(vmem_limit_bytes=mebibytes << 20)


def held(space, *arrays):
    return [pltpu.with_memory_space_constraint(a, space) for a in arrays]


def divisor(total, most, unit):
    fits = [n for n in range(unit, min(total, most) + 1, unit) if total % n == 0]
    return fits[-1] if fits else total


def attend_kernel(
    length_ref,
    query_ref,
    keys_hbm,
    values_hbm,
    new_keys_ref,
    new_values_ref,
    resident_hbm,
    out_ref,
    cut_hbm,
    keys_ref,
    values_ref,
    past_ref,
    own_ref,
    cut_ref,
    sems,
    *,
    width,
):
    row = pl.program_id(0)
    steps, features = query_ref.shape[1:]
    _, kv_features = keys_ref.shape
    grouping = features // kv_features
    heads = width // HD
    bands = kv_features // width
    block_rows = grouping * steps
    rows = heads * block_rows
    factor = HD ** (-0.5)
    load_keys, load_values = [], []
    for band in range(bands):
        at = pl.ds(band * width, width)
        load_keys.append(pltpu.make_async_copy(keys_hbm.at[row, :, at], keys_ref.at[:, at], sems.at[band]))
        load_values.append(
            pltpu.make_async_copy(values_hbm.at[row, :, at], values_ref.at[:, at], sems.at[bands + band])
        )
    for copy in load_keys + load_values:
        copy.start()
    blocks = cut_hbm.shape[0]
    part = pl.ds(lax.axis_index("dp") * blocks, blocks)
    cut_in = pltpu.make_async_copy(resident_hbm.at[part], cut_ref, sems.at[2 * bands])
    cut_out = pltpu.make_async_copy(cut_ref, cut_hbm, sems.at[2 * bands + 1])
    cut_in.start()

    query = query_ref[0].astype(jnp.float32)
    padding = jnp.zeros((8 - steps % 8, kv_features), jnp.float32)
    keys_new = jnp.concatenate([new_keys_ref[0].astype(jnp.float32), padding], axis=0).astype(jnp.bfloat16)
    values_new = jnp.concatenate([new_values_ref[0].astype(jnp.float32), padding], axis=0).astype(jnp.bfloat16)
    stacks = []
    for band in range(bands):
        lines = []
        for k in range(heads):
            first = (band * heads + k) * grouping
            pieces = [query[:, (first + g) * HD : (first + g + 1) * HD] for g in range(grouping)]
            own = jnp.concatenate(pieces, axis=0)
            lines.append(jnp.concatenate([own if i == k else jnp.zeros_like(own) for i in range(heads)], axis=1))
        stacks.append(jnp.concatenate(lines, axis=0).astype(jnp.bfloat16))
    for band in range(bands):
        at = slice(band * width, (band + 1) * width)
        own_ref[band * rows : (band + 1) * rows] = dot(stacks[band], keys_new[:, at], NT)
    for band in range(bands):
        at = slice(band * width, (band + 1) * width)
        load_keys[band].wait()
        past_ref[band * rows : (band + 1) * rows] = dot(stacks[band], keys_ref[:, at], NT)

    cut_in.wait()
    cut_out.start()
    past = past_ref[...] * factor
    own = own_ref[...] * factor
    slot = lax.broadcasted_iota(jnp.int32, past.shape, 1)
    past = jnp.where(slot < length_ref[row], past, -jnp.inf)
    column = lax.broadcasted_iota(jnp.int32, own.shape, 1)
    position = lax.rem(lax.broadcasted_iota(jnp.int32, own.shape, 0), steps)
    own = jnp.where(column <= position, own, -jnp.inf)
    highest = jnp.maximum(jnp.max(past, axis=1, keepdims=True), jnp.max(own, axis=1, keepdims=True))
    past = jnp.exp(past - highest)
    own = jnp.exp(own - highest)
    scale = 1.0 / (jnp.sum(past, axis=1, keepdims=True) + jnp.sum(own, axis=1, keepdims=True))
    past = (past * scale).astype(jnp.bfloat16)
    own = (own * scale).astype(jnp.bfloat16)

    for band in range(bands):
        at = slice(band * width, (band + 1) * width)
        lines = slice(band * rows, (band + 1) * rows)
        load_values[band].wait()
        attended = dot(past[lines], values_ref[:, at], NN) + dot(own[lines], values_new[:, at], NN)
        for k in range(heads):
            for g in range(grouping):
                head = (band * heads + k) * grouping + g
                piece = k * block_rows + g * steps
                value = attended[piece : piece + steps, k * HD : (k + 1) * HD].astype(jnp.bfloat16)
                for copy in range(out_ref.shape[0]):
                    out_ref[copy, 0, :, head * HD : (head + 1) * HD] = value
    cut_out.wait()


def attend(query, cache_keys, cache_values, new_keys, new_values, cache_lengths, stored, blocks, copies):
    rows, steps, features = query.shape
    slots, kv_features = cache_keys.shape[1:]
    width = HD * 2 if kv_features % (HD * 2) == 0 else HD
    bands = kv_features // width
    lines = features // HD * steps
    one = lambda s: pl.BlockSpec((1, *s[1:]), lambda r, *_: (r, 0, 0))
    hbm = pl.BlockSpec(memory_space=pltpu.HBM)
    return pl.pallas_call(
        functools.partial(attend_kernel, width=width),
        out_shape=[
            jax.ShapeDtypeStruct((copies, *query.shape), jnp.bfloat16),
            jax.ShapeDtypeStruct((blocks, *stored.shape[1:]), stored.dtype),
        ],
        grid_spec=pltpu.PrefetchScalarGridSpec(
            num_scalar_prefetch=1,
            grid=(rows,),
            in_specs=[one(query.shape), hbm, hbm, one(new_keys.shape), one(new_values.shape), hbm],
            out_specs=[pl.BlockSpec((copies, 1, steps, features), lambda r, *_: (0, r, 0, 0)), hbm],
            scratch_shapes=[
                pltpu.VMEM((slots, kv_features), cache_keys.dtype),
                pltpu.VMEM((slots, kv_features), cache_values.dtype),
                pltpu.VMEM((lines, slots), jnp.float32),
                pltpu.VMEM((lines, 8 * (steps // 8 + 1)), jnp.float32),
                pltpu.VMEM((blocks, *stored.shape[1:]), stored.dtype),
                pltpu.SemaphoreType.DMA((2 * bands + 2,)),
            ],
        ),
        compiler_params=limit(16),
        name="attend",
    )(cache_lengths, *held(pltpu.HBM, query, cache_keys, cache_values, new_keys, new_values, stored))


def change_kernel(new_hbm, synced_hbm, out_hbm, new_ref, synced_ref, out_ref, sems, *, take):
    blocks, rows, depth = out_ref.shape
    loads, stores = [], []
    for i in range(rows // take):
        at = pl.ds(i * take, take)
        loads.append(
            (
                pltpu.make_async_copy(new_hbm.at[at], new_ref.at[at], sems.at[3 * i]),
                pltpu.make_async_copy(synced_hbm.at[at], synced_ref.at[at], sems.at[3 * i + 1]),
            )
        )
        stores.append(pltpu.make_async_copy(out_ref.at[:, at], out_hbm.at[:, at], sems.at[3 * i + 2]))
        loads[i][0].start()
        loads[i][1].start()
    for i, pair in enumerate(loads):
        pair[0].wait()
        pair[1].wait()
        at = slice(i * take, (i + 1) * take)
        for b in range(blocks):
            columns = slice(b * depth, (b + 1) * depth)
            out_ref[b, at] = (new_ref[at, columns] - synced_ref[at, columns]).astype(jnp.bfloat16)
        stores[i].start()
    for store in stores:
        store.wait()


def local_change(new_weight, synced_weight, blocks):
    rows, features = new_weight.shape
    take = divisor(rows, 24, 8)
    hbm = pl.BlockSpec(memory_space=pltpu.HBM)
    cut = (blocks, rows, features // blocks)
    return pl.pallas_call(
        functools.partial(change_kernel, take=take),
        out_shape=jax.ShapeDtypeStruct(cut, jnp.bfloat16),
        in_specs=[hbm] * 2,
        out_specs=hbm,
        scratch_shapes=[
            pltpu.VMEM((rows, features), jnp.float32),
            pltpu.VMEM((rows, features), jnp.float32),
            pltpu.VMEM(cut, jnp.bfloat16),
            pltpu.SemaphoreType.DMA((3 * (rows // take),)),
        ],
        compiler_params=limit(24),
        name="local_change",
    )(*held(pltpu.HBM, new_weight, synced_weight))


def project_kernel(*refs, parts):
    gathered = refs[:parts]
    change_ref, *weights_hbm = refs[parts : parts + 4]
    out_ref, weights_ref, rows_ref, sums_ref, sems = refs[parts + 4 :]
    owners, steps, _ = out_ref.shape
    blocks, _, depth = change_ref.shape
    device = lax.axis_index("tensor")
    places = (device, device ^ 1)
    group = lax.axis_index("dp") if parts > 1 else 0
    loads = [pltpu.make_async_copy(weights_hbm[w], weights_ref.at[w], sems.at[w]) for w in range(3)]
    for load in loads:
        load.start()

    pieces = []
    for part in gathered:
        for k in range(part.shape[0]):
            pieces.append(part[k].astype(jnp.float32))
    rows_ref[...] = jnp.concatenate(pieces, axis=0).astype(jnp.bfloat16)

    def of_change(ref):
        value = dot(ref[0], rows_ref[:, :depth], NT)
        for b in range(1, blocks):
            value += dot(ref[b], rows_ref[:, b * depth : (b + 1) * depth], NT)
        return value

    own = of_change(change_ref)
    for source, w in enumerate((0, 1)):
        loads[w].wait()
        rows = rows_ref[:, pl.ds(pl.multiple_of(places[source] * depth, depth), depth)]
        for b in range(blocks):
            value = dot(weights_ref[w, b], rows, NT)
            if source == 0:
                sums_ref[b] = value
            else:
                sums_ref[b] += value
    loads[2].wait()
    other = of_change(weights_ref.at[2])
    sums_ref[places[0]] += own
    sums_ref[places[1]] += other
    sums = jnp.concatenate([sums_ref[b] for b in range(blocks)], axis=0).T
    each = owners // parts
    for k in range(owners):
        owner = (group ^ (k // each)) * each + k % each
        out_ref[owner] = sums[k * steps : (k + 1) * steps]


def project(gathered, weights, owners, steps):
    blocks, width, depth = weights[0].shape
    take = owners if len(gathered) > 1 else divisor(owners, MOST, 1)
    several = owners > take
    whole = pl.BlockSpec(memory_space=pltpu.VMEM)
    cut = lambda s: pl.BlockSpec((take, *s[1:]), lambda i: (i, 0, 0)) if several else whole
    out = jax.ShapeDtypeStruct((owners, steps, blocks * width), jnp.float32)
    return pl.pallas_call(
        functools.partial(project_kernel, parts=len(gathered)),
        out_shape=out,
        grid=(owners // take,),
        in_specs=[*[cut(g.shape) for g in gathered], whole, *[pl.BlockSpec(memory_space=pltpu.HBM)] * 3],
        out_specs=cut(out.shape),
        scratch_shapes=[
            pltpu.VMEM((3, blocks, width, depth), jnp.bfloat16),
            pltpu.VMEM((take * steps, blocks * depth), jnp.bfloat16),
            pltpu.VMEM((blocks, width, take * steps), jnp.float32),
            pltpu.SemaphoreType.DMA((3,)),
        ],
        compiler_params=limit(24 if not several else 40),
        name="project",
    )(
        *(gathered if several else held(pltpu.VMEM, *gathered)),
        *held(pltpu.VMEM, weights[0]),
        *held(pltpu.HBM, *weights[1:]),
    )


def norm_kernel(partial_ref, gain_ref, out_ref, sums_ref, *, groups):
    owners, _, columns = partial_ref.shape
    count = out_ref.shape[0]
    chips = owners // groups // count
    for r in range(count):
        for d in range(groups):
            value = partial_ref[d * chips * count + r]
            for z in range(1, chips):
                value += partial_ref[(d * chips + z) * count + r]
            sums_ref[:, d * columns : (d + 1) * columns] = value
        projected = sums_ref[...]
        mean_square = jnp.mean(projected * projected, axis=1, keepdims=True)
        out_ref[r] = (projected * lax.rsqrt(mean_square + 1e-06) * gain_ref[...]).astype(jnp.bfloat16)


def normalise(partial, gain, groups, count):
    steps, columns = partial.shape[1], partial.shape[2] * groups
    return pl.pallas_call(
        functools.partial(norm_kernel, groups=groups),
        out_shape=jax.ShapeDtypeStruct((count, steps, columns), jnp.bfloat16),
        in_specs=[pl.BlockSpec(memory_space=pltpu.VMEM)] * 2,
        out_specs=pl.BlockSpec(memory_space=pltpu.VMEM),
        scratch_shapes=[pltpu.VMEM((steps, columns), jnp.float32)],
        compiler_params=limit(8),
        name="normalise",
    )(partial, gain.reshape(1, columns))


def body(
    new_weight,
    synced_weight,
    resident,
    gain,
    query,
    cache_keys,
    cache_values,
    new_keys,
    new_values,
    cache_lengths,
):
    groups, devices = lax.axis_size("dp"), lax.axis_size("tensor")
    chips = devices // CORES
    count, steps, features = query.shape

    def exchange(value, axis, size, hop):
        return lax.ppermute(value, axis, [(i, i ^ hop) for i in range(size)])

    stored = resident.reshape(groups * devices, -1, resident.shape[1])
    copies, cut = attend(query, cache_keys, cache_values, new_keys, new_values, cache_lengths, stored, devices, chips)
    column = lax.all_to_all(
        copies.reshape(chips * count, steps, features),
        "tensor",
        split_axis=0,
        concat_axis=0,
        tiled=True,
        axis_index_groups=[[i * CORES + c for i in range(chips)] for c in range(CORES)],
    )
    change = local_change(new_weight, synced_weight, devices)
    weights = [change, cut, exchange(cut, "tensor", devices, 1), exchange(change, "tensor", devices, 1)]
    if groups <= FEW and groups & (groups - 1) == 0:
        gathered = [column]
        for hop in range(1, groups):
            gathered.append(exchange(column, "dp", groups, hop))
    else:
        gathered = [lax.all_gather(column, "dp", axis=0, tiled=True)]
    partial = project(gathered, weights, groups * chips * count, steps)
    summed = lax.all_to_all(
        partial,
        ("dp", "tensor"),
        split_axis=0,
        concat_axis=0,
        tiled=True,
        axis_index_groups=[
            [g * devices + i * CORES + c for g in range(groups) for i in range(chips)] for c in range(CORES)
        ],
    )
    return normalise(summed, gain, groups, count)


def solution(mesh):
    in_specs = (
        P(("dp", "tensor"), None),
        P(("dp", "tensor"), None),
        P(None, "tensor"),
        P(),
        P(("dp", "tensor"), None, None),
        P(("dp", "tensor"), None, None),
        P(("dp", "tensor"), None, None),
        P(("dp", "tensor"), None, None),
        P(("dp", "tensor"), None, None),
        P(("dp", "tensor")),
    )
    out_specs = P(("dp", "tensor"), None, None)
    return jax.shard_map(body, mesh=mesh, in_specs=in_specs, out_specs=out_specs, check_vma=False)
```

time: 60.8 us -> 55.2 us (0.908)
  blocking collectives: 0 us -> 12.1 us
  Pallas kernels: 25.3 us -> 16.9 us
  waiting for transfers between devices: 18 us -> 13.3 us
  starting transfers between devices: 12.7 us -> 8.65 us
  other arithmetic: 0.99 us -> 0 us
    all_to_all x0 -> x1, blocking collectives: none -> 12.1 us  [body(): lax.all_to_all(copies.reshape(chips * count, steps, features), 'tensor',...]
    ppermute x7 -> x5, waiting for transfers between devices: 10.9 us -> 5.56 us  [exchange(): return lax.ppermute(value, axis, [(i, i ^ hop) for i in range(size)])]
    ppermute x7 -> x5, starting transfers between devices: 9.2 us -> 4.65 us  [exchange(): return lax.ppermute(value, axis, [(i, i ^ hop) for i in range(size)])]
    pallas_call x2, Pallas kernels: 14.2 us -> 10.1 us  [the longest x1 5.26 us: attend(): pl.pallas_call(functools.partial(attend_kernel, width=width), out_shape=[...]
    pallas_call x1, Pallas kernels: 9.34 us -> 6 us  [project(): pl.pallas_call(functools.partial(project_kernel, parts=len(gathered)), ou...]
    unnamed x12 -> x8, local copies, waits for them, and re-layouts: 1.34 us -> 3.13 us
    concatenate x1 -> x0, other arithmetic: 0.99 us -> none  [body(): jnp.concatenate([attended] + [exchange(attended, 'tensor', devices, CORES...]
    pallas_call x1, Pallas kernels: 1.75 us -> 0.83 us  [normalise(): pl.pallas_call(functools.partial(norm_kernel, groups=groups), out_shape=j...]
  transfers between devices with their start and end apart: 8 -> 6, of which waited for: 5 -> 3; matrix products, arithmetic and copies ran while one was open for 4% -> 0% of each run, Pallas kernels for 8% -> 9%
where the time goes in v2:
time: 55.2 us; the launch traced here: 54.9 us
  Pallas kernels  16.9 us (31%)
  waiting for transfers between devices  13.3 us (24%)
  blocking collectives  12.1 us (22%)
  starting transfers between devices  8.65 us (16%)
  local copies, waits for them, and re-layouts  3.14 us (6%)
  between operations  0.73 us (1%)
    all_to_all x1, blocking collectives, body(): lax.all_to_all(copies.reshape(chips * count, steps, features), 'tensor',...  12.1 us
    all_to_all x1, waiting for transfers between devices, body(): lax.all_to_all(partial, ('dp', 'tensor'), split_axis=0, concat_axis=0, ti...  7.78 us
    pallas_call x1, Pallas kernels, project(): pl.pallas_call(functools.partial(project_kernel, parts=len(gathered)), ou...  6 us
    ppermute x5, waiting for transfers between devices, exchange(): return lax.ppermute(value, axis, [(i, i ^ hop) for i in range(size)])  5.56 us
    pallas_call x1, Pallas kernels, attend(): pl.pallas_call(functools.partial(attend_kernel, width=width), out_shape=[...  5.26 us
    pallas_call x1, Pallas kernels, local_change(): pl.pallas_call(functools.partial(change_kernel, take=take), out_shape=jax...  4.83 us
    ppermute x5, starting transfers between devices, exchange(): return lax.ppermute(value, axis, [(i, i ^ hop) for i in range(size)])  4.65 us
    all_to_all x1, starting transfers between devices, body(): lax.all_to_all(partial, ('dp', 'tensor'), split_axis=0, concat_axis=0, ti...  4 us
  transfers between devices with their start and end apart: 6, of which 3 were waited for; matrix products, arithmetic and copies ran while one was open for 0% of the time, Pallas kernels for 9%

profile of v2, /device:TPU:0, one launch (start us, length us, event | category | flops | bytes accessed | tf_op | source)
XLA Modules:
  0.0 54.9 jit_solution(12185703688582847728)
XLA Ops:
  0.7 5.3 %attend.1 = (bf16[4,1,2,8192]{3,2,1,0:T(2,128)(2,1)S(1)}, bf16[8,168,1024]{2,1,0:T(8,128)(2,1)S(1)}) custom-call(s32[1]{0:T(128)S(6)} %copy.11.length_ref, bf16[1,2,8192]{2,1,0:T(2,128)(2,1)} %query_ref.1, bf16[1,768,1024]{2,1,0:T(8,128)(2,1)} %keys_hbm.1, bf16[1,768,1024]{2,1,0:T(8,128)(2,1)} %values_hbm.1, bf16[1,2,1024]{2,1,0:T(2,128)(2,1)} %new_keys_ref.1, ...), custom_call_target="tpu_custom_call" | custom-call | tf_op jit(solution)/shard_map/attend/pallas_call | solution.py:139
  5.9 0.0 copy-start
  5.9 0.6 %collective-permute-start.3 = (bf16[8,168,1024]{2,1,0:T(8,128)(2,1)S(1)}, bf16[8,168,1024]{2,1,0:T(8,128)(2,1)S(1)}, u32[]{:S(2)}, u32[]{:S(2)}) collective-permute-start(bf16[8,168,1024]{2,1,0:T(8,128)(2,1)S(1)} %get-tuple-element.8.refs_5_), channel_id=1, source_target_pairs={{0,1},{1,0},{2,3},{3,2},{4,5},{5,4},{6,7},{7,6},{8,9},{9,8},{10,11... | collective-permute-start | bytes 8257544 | tf_op jit(solution)/shard_map/ppermute | solution.py:330
  6.5 4.8 %local_change.1.refs_4_ = bf16[8,168,1024]{2,1,0:T(8,128)(2,1)S(1)} custom-call(f32[168,8192]{1,0:T(8,128)} %new_hbm.1, f32[168,8192]{1,0:T(8,128)} %synced_hbm.1), custom_call_target="tpu_custom_call" | custom-call | tf_op jit(solution)/shard_map/local_change/pallas_call | solution.py:195
  11.3 0.0 copy-done
  11.3 0.6 %collective-permute-start.4 = (bf16[8,168,1024]{2,1,0:T(8,128)(2,1)S(1)}, bf16[8,168,1024]{2,1,0:T(8,128)(2,1)S(1)}, u32[]{:S(2)}, u32[]{:S(2)}) collective-permute-start(bf16[8,168,1024]{2,1,0:T(8,128)(2,1)S(1)} %local_change.1.refs_4_), channel_id=1, source_target_pairs={{0,1},{1,0},{2,3},{3,2},{4,5},{5,4},{6,7},{7,6},{8,9},{9,8},{10,11... | collective-permute-start | bytes 8257544 | tf_op jit(solution)/shard_map/ppermute | solution.py:330
  11.9 12.1 %all_to_all.10.refs_0_ = bf16[4,2,8192]{2,1,0:T(2,128)(2,1)S(1)} all-to-all(bf16[4,2,8192]{2,1,0:T(2,128)(2,1)S(1)} %bitcast.2), channel_id=1, replica_groups={{0,2,4,6},{1,3,5,7},{8,10,12,14},{9,11,13,15},{16,18,20,22},{17,19,21,2..., dimensions={0} | all-to-all | bytes 262144 | tf_op jit(solution)/shard_map/all_to_all | solution.py:334
  24.0 0.0 copy-start.3
  24.0 1.5 %collective-permute-start = (bf16[4,2,8192]{2,1,0:T(2,128)(2,1)S(1)}, bf16[4,2,8192]{2,1,0:T(2,128)(2,1)S(1)}, u32[]{:S(2)}, u32[]{:S(2)}) collective-permute-start(bf16[4,2,8192]{2,1,0:T(2,128)(2,1)S(1)} %all_to_all.10.refs_0_), channel_id=1, source_target_pairs={{0,8},{8,0},{16,24},{24,16},{1,9},{9,1},{17,25},{25,17},{2,10},{10... | collective-permute-start | bytes 393224 | tf_op jit(solution)/shard_map/ppermute | solution.py:330
  25.5 1.5 %collective-permute-start.1 = (bf16[4,2,8192]{2,1,0:T(2,128)(2,1)S(1)}, bf16[4,2,8192]{2,1,0:T(2,128)(2,1)S(1)}, u32[]{:S(2)}, u32[]{:S(2)}) collective-permute-start(bf16[4,2,8192]{2,1,0:T(2,128)(2,1)S(1)} %all_to_all.10.refs_0_), channel_id=1, source_target_pairs={{0,16},{8,24},{16,0},{24,8},{1,17},{9,25},{17,1},{25,9},{2,18},{10... | collective-permute-start | bytes 393224 | tf_op jit(solution)/shard_map/ppermute | solution.py:330
  27.0 0.5 collective-permute-start.2
  27.5 2.8 %collective-permute-done.refs_1_ = bf16[4,2,8192]{2,1,0:T(2,128)(2,1)S(1)} collective-permute-done((bf16[4,2,8192]{2,1,0:T(2,128)(2,1)S(1)}, bf16[4,2,8192]{2,1,0:T(2,128)(2,1)S(1)}, u32[]{:S(2)}, u32[]{:S(2)}) %collective-permute-start) | collective-permute-done | bytes 131104 | tf_op jit(solution)/shard_map/ppermute | solution.py:330
  30.3 2.7 %collective-permute-done.1.refs_2_ = bf16[4,2,8192]{2,1,0:T(2,128)(2,1)S(1)} collective-permute-done((bf16[4,2,8192]{2,1,0:T(2,128)(2,1)S(1)}, bf16[4,2,8192]{2,1,0:T(2,128)(2,1)S(1)}, u32[]{:S(2)}, u32[]{:S(2)}) %collective-permute-start.1) | collective-permute-done | bytes 131104 | tf_op jit(solution)/shard_map/ppermute | solution.py:330
  33.1 0.0 collective-permute-done.2.refs_3_
  33.1 0.0 collective-permute-done.3.refs_6_
  33.1 0.0 copy-start.1
  33.1 0.0 collective-permute-done.4.refs_7_
  33.1 1.6 %copy-done.1 = bf16[8,168,1024]{2,1,0:T(8,128)(2,1)} copy-done((bf16[8,168,1024]{2,1,0:T(8,128)(2,1)}, bf16[8,168,1024]{2,1,0:T(8,128)(2,1)S(1)}, u32[]{:S(2)}) %copy-start.1) | copy-done | bytes 2752536
  34.7 0.0 copy-start.2
  34.7 1.5 %copy-done.2 = bf16[8,168,1024]{2,1,0:T(8,128)(2,1)} copy-done((bf16[8,168,1024]{2,1,0:T(8,128)(2,1)}, bf16[8,168,1024]{2,1,0:T(8,128)(2,1)S(1)}, u32[]{:S(2)}) %copy-start.2) | copy-done | bytes 2752536
  36.2 6.0 %project.1 = f32[16,2,1344]{2,1,0:T(2,128)} custom-call(bf16[4,2,8192]{2,1,0:T(2,128)(2,1)S(1)} %all_to_all.10.refs_0_, bf16[4,2,8192]{2,1,0:T(2,128)(2,1)S(1)} %collective-permute-done.refs_1_, bf16[4,2,8192]{2,1,0:T(2,128)(2,1)S(1)} %collective-permute-done.1.refs_2_, bf16[4,2,8192]{2,1,0:T(2,128)(2,1)S(1)} %collective-permute-done.2.refs_3_, ...), custom_call_target="tpu_custom_call" | custom-call | tf_op jit(solution)/shard_map/project/pallas_call | solution.py:264
  42.2 4.0 %all-to-all-start.1 = ((f32[16,2,1344]{2,1,0:T(2,128)}), f32[16,2,1344]{2,1,0:T(2,128)S(1)}, u32[]{:S(2)}, u32[]{:S(2)}) async-start(f32[16,2,1344]{2,1,0:T(2,128)} %project.1), calls=%async_computation.1 | async-start | bytes 360448 | tf_op jit(solution)/shard_map/all_to_all | solution.py:351
  46.2 0.0 copy-done.3
  46.3 7.8 %all-to-all-done.1.partial_ref = f32[16,2,1344]{2,1,0:T(2,128)S(1)} async-done(((f32[16,2,1344]{2,1,0:T(2,128)}), f32[16,2,1344]{2,1,0:T(2,128)S(1)}, u32[]{:S(2)}, u32[]{:S(2)}) %all-to-all-start.1) | async-done | bytes 172064 | tf_op jit(solution)/shard_map/all_to_all | solution.py:351
  54.0 0.8 %normalise.1 = bf16[1,2,5376]{2,1,0:T(2,128)(2,1)} custom-call(f32[16,2,1344]{2,1,0:T(2,128)S(1)} %all-to-all-done.1.partial_ref, f32[1,5376]{1,0:T(1,128)S(1)} %reshape.11.gain_ref), custom_call_target="tpu_custom_call" | custom-call | tf_op jit(solution)/shard_map/normalise/pallas_call | solution.py:302
  (1 shorter events, 0.0 us)
Async XLA Ops:
  5.9 5.4 %copy-start = (bf16[8,168,1024]{2,1,0:T(8,128)(2,1)}, bf16[8,168,1024]{2,1,0:T(8,128)(2,1)S(1)}, u32[]{:S(2)}) copy-start(bf16[8,168,1024]{2,1,0:T(8,128)(2,1)S(1)} %get-tuple-element.8.refs_5_) | copy-start | bytes 8257540
  5.9 27.2 %collective-permute-start.3 = (bf16[8,168,1024]{2,1,0:T(8,128)(2,1)S(1)}, bf16[8,168,1024]{2,1,0:T(8,128)(2,1)S(1)}, u32[]{:S(2)}, u32[]{:S(2)}) collective-permute-start(bf16[8,168,1024]{2,1,0:T(8,128)(2,1)S(1)} %get-tuple-element.8.refs_5_), channel_id=1, source_target_pairs={{0,1},{1,0},{2,3},{3,2},{4,5},{5,4},{6,7},{7,6},{8,9},{9,8},{10,11... | collective-permute-start | bytes 8257544 | tf_op jit(solution)/shard_map/ppermute | solution.py:330
  11.3 21.8 %collective-permute-start.4 = (bf16[8,168,1024]{2,1,0:T(8,128)(2,1)S(1)}, bf16[8,168,1024]{2,1,0:T(8,128)(2,1)S(1)}, u32[]{:S(2)}, u32[]{:S(2)}) collective-permute-start(bf16[8,168,1024]{2,1,0:T(8,128)(2,1)S(1)} %local_change.1.refs_4_), channel_id=1, source_target_pairs={{0,1},{1,0},{2,3},{3,2},{4,5},{5,4},{6,7},{7,6},{8,9},{9,8},{10,11... | collective-permute-start | bytes 8257544 | tf_op jit(solution)/shard_map/ppermute | solution.py:330
  24.0 22.2 %copy-start.3 = (f32[5376]{0:T(1024)S(1)}, f32[5376]{0:T(1024)}, u32[]{:S(2)}) copy-start(f32[5376]{0:T(1024)} %param.13) | copy-start | bytes 64516
  24.0 6.3 %collective-permute-start = (bf16[4,2,8192]{2,1,0:T(2,128)(2,1)S(1)}, bf16[4,2,8192]{2,1,0:T(2,128)(2,1)S(1)}, u32[]{:S(2)}, u32[]{:S(2)}) collective-permute-start(bf16[4,2,8192]{2,1,0:T(2,128)(2,1)S(1)} %all_to_all.10.refs_0_), channel_id=1, source_target_pairs={{0,8},{8,0},{16,24},{24,16},{1,9},{9,1},{17,25},{25,17},{2,10},{10... | collective-permute-start | bytes 393224 | tf_op jit(solution)/shard_map/ppermute | solution.py:330
  25.5 7.5 %collective-permute-start.1 = (bf16[4,2,8192]{2,1,0:T(2,128)(2,1)S(1)}, bf16[4,2,8192]{2,1,0:T(2,128)(2,1)S(1)}, u32[]{:S(2)}, u32[]{:S(2)}) collective-permute-start(bf16[4,2,8192]{2,1,0:T(2,128)(2,1)S(1)} %all_to_all.10.refs_0_), channel_id=1, source_target_pairs={{0,16},{8,24},{16,0},{24,8},{1,17},{9,25},{17,1},{25,9},{2,18},{10... | collective-permute-start | bytes 393224 | tf_op jit(solution)/shard_map/ppermute | solution.py:330
  27.0 6.0 %collective-permute-start.2 = (bf16[4,2,8192]{2,1,0:T(2,128)(2,1)S(1)}, bf16[4,2,8192]{2,1,0:T(2,128)(2,1)S(1)}, u32[]{:S(2)}, u32[]{:S(2)}) collective-permute-start(bf16[4,2,8192]{2,1,0:T(2,128)(2,1)S(1)} %all_to_all.10.refs_0_), channel_id=1, source_target_pairs={{0,24},{8,16},{16,8},{24,0},{1,25},{9,17},{17,9},{25,1},{2,26},{10... | collective-permute-start | bytes 393224 | tf_op jit(solution)/shard_map/ppermute | solution.py:330
  33.1 1.6 %copy-start.1 = (bf16[8,168,1024]{2,1,0:T(8,128)(2,1)}, bf16[8,168,1024]{2,1,0:T(8,128)(2,1)S(1)}, u32[]{:S(2)}) copy-start(bf16[8,168,1024]{2,1,0:T(8,128)(2,1)S(1)} %collective-permute-done.3.refs_6_) | copy-start | bytes 8257540
  34.7 1.5 %copy-start.2 = (bf16[8,168,1024]{2,1,0:T(8,128)(2,1)}, bf16[8,168,1024]{2,1,0:T(8,128)(2,1)S(1)}, u32[]{:S(2)}) copy-start(bf16[8,168,1024]{2,1,0:T(8,128)(2,1)S(1)} %collective-permute-done.4.refs_7_) | copy-start | bytes 8257540
  42.2 11.8 %all-to-all-start.1 = ((f32[16,2,1344]{2,1,0:T(2,128)}), f32[16,2,1344]{2,1,0:T(2,128)S(1)}, u32[]{:S(2)}, u32[]{:S(2)}) async-start(f32[16,2,1344]{2,1,0:T(2,128)} %project.1), calls=%async_computation.1 | async-start | bytes 360448 | tf_op jit(solution)/shard_map/all_to_all | solution.py:351

commit v3 on v2

v3 whole, which is shorter than its diff:
```python
import functools

import jax
import jax.numpy as jnp
from jax import lax
from jax.experimental import pallas as pl
from jax.experimental.pallas import tpu as pltpu
from jax.sharding import PartitionSpec as P


HD = 128
CORES = 2
MOST = 32
FEW = 4
NT = (((1,), (1,)), ((), ()))
NN = (((1,), (0,)), ((), ()))


def dot(a, b, dims):
    return lax.dot_general(a, b, dims, preferred_element_type=jnp.float32)


def limit(mebibytes):
    return pltpu.CompilerParams(vmem_limit_bytes=mebibytes << 20)


def held(space, *arrays):
    return [pltpu.with_memory_space_constraint(a, space) for a in arrays]


def divisor(total, most, unit):
    fits = [n for n in range(unit, min(total, most) + 1, unit) if total % n == 0]
    return fits[-1] if fits else total


def attend_kernel(
    lengths_ref,
    query_hbm,
    keys_hbm,
    values_hbm,
    new_keys_hbm,
    new_values_hbm,
    out_hbm,
    query_ref,
    keys_ref,
    values_ref,
    new_keys_ref,
    new_values_ref,
    past_ref,
    own_ref,
    out_ref,
    sems,
    *,
    width,
):
    count, steps, features = query_hbm.shape
    _, kv_features = keys_ref.shape
    grouping = features // kv_features
    heads = width // HD
    bands = kv_features // width
    block_rows = grouping * steps
    rows = heads * block_rows
    factor = HD ** (-0.5)
    for row in range(count):
        pairs = [
            (query_hbm, query_ref),
            (new_keys_hbm, new_keys_ref),
            (keys_hbm, keys_ref),
            (new_values_hbm, new_values_ref),
            (values_hbm, values_ref),
        ]
        loads = [pltpu.make_async_copy(p[0].at[row], p[1], sems.at[i]) for i, p in enumerate(pairs)]
        for load in loads:
            load.start()

        padding = jnp.zeros((8 - steps % 8, kv_features), jnp.float32)
        loads[0].wait()
        query = query_ref[...].astype(jnp.float32)
        stacks = []
        for band in range(bands):
            lines = []
            for k in range(heads):
                first = (band * heads + k) * grouping
                pieces = [query[:, (first + g) * HD : (first + g + 1) * HD] for g in range(grouping)]
                own = jnp.concatenate(pieces, axis=0)
                lines.append(jnp.concatenate([own if i == k else jnp.zeros_like(own) for i in range(heads)], axis=1))
            stacks.append(jnp.concatenate(lines, axis=0).astype(jnp.bfloat16))
        loads[1].wait()
        keys_new = jnp.concatenate([new_keys_ref[...].astype(jnp.float32), padding], axis=0).astype(jnp.bfloat16)
        for band in range(bands):
            at = slice(band * width, (band + 1) * width)
            own_ref[band * rows : (band + 1) * rows] = dot(stacks[band], keys_new[:, at], NT)
        loads[2].wait()
        for band in range(bands):
            at = slice(band * width, (band + 1) * width)
            past_ref[band * rows : (band + 1) * rows] = dot(stacks[band], keys_ref[:, at], NT)

        past = past_ref[...] * factor
        own = own_ref[...] * factor
        slot = lax.broadcasted_iota(jnp.int32, past.shape, 1)
        past = jnp.where(slot < lengths_ref[row], past, -jnp.inf)
        column = lax.broadcasted_iota(jnp.int32, own.shape, 1)
        position = lax.rem(lax.broadcasted_iota(jnp.int32, own.shape, 0), steps)
        own = jnp.where(column <= position, own, -jnp.inf)
        highest = jnp.maximum(jnp.max(past, axis=1, keepdims=True), jnp.max(own, axis=1, keepdims=True))
        past = jnp.exp(past - highest)
        own = jnp.exp(own - highest)
        scale = 1.0 / (jnp.sum(past, axis=1, keepdims=True) + jnp.sum(own, axis=1, keepdims=True))
        past = (past * scale).astype(jnp.bfloat16)
        own = (own * scale).astype(jnp.bfloat16)

        loads[3].wait()
        values_new = jnp.concatenate([new_values_ref[...].astype(jnp.float32), padding], axis=0).astype(jnp.bfloat16)
        loads[4].wait()
        for band in range(bands):
            at = slice(band * width, (band + 1) * width)
            lines = slice(band * rows, (band + 1) * rows)
            attended = dot(past[lines], values_ref[:, at], NN) + dot(own[lines], values_new[:, at], NN)
            for k in range(heads):
                for g in range(grouping):
                    head = (band * heads + k) * grouping + g
                    piece = k * block_rows + g * steps
                    value = attended[piece : piece + steps, k * HD : (k + 1) * HD]
                    out_ref[:, head * HD : (head + 1) * HD] = value.astype(jnp.bfloat16)
        stores = [
            pltpu.make_async_copy(out_ref, out_hbm.at[copy, row], sems.at[5 + copy])
            for copy in range(out_hbm.shape[0])
        ]
        for store in stores:
            store.start()
        for store in stores:
            store.wait()


def attend(query, cache_keys, cache_values, new_keys, new_values, cache_lengths, copies):
    _, steps, features = query.shape
    slots, kv_features = cache_keys.shape[1:]
    width = HD * 2 if kv_features % (HD * 2) == 0 else HD
    lines = features // HD * steps
    hbm = pl.BlockSpec(memory_space=pltpu.HBM)
    operands = held(pltpu.HBM, query, cache_keys, cache_values, new_keys, new_values)
    return pl.pallas_call(
        functools.partial(attend_kernel, width=width),
        out_shape=jax.ShapeDtypeStruct((copies, *query.shape), query.dtype),
        in_specs=[pl.BlockSpec(memory_space=pltpu.SMEM), *[hbm] * len(operands)],
        out_specs=hbm,
        scratch_shapes=[
            *[pltpu.VMEM(o.shape[1:], o.dtype) for o in operands],
            pltpu.VMEM((lines, slots), jnp.float32),
            pltpu.VMEM((lines, 8 * (steps // 8 + 1)), jnp.float32),
            pltpu.VMEM(query.shape[1:], query.dtype),
            pltpu.SemaphoreType.DMA((5 + copies,)),
        ],
        compiler_params=limit(16),
        name="attend",
    )(cache_lengths, *operands)


def change_kernel(new_hbm, synced_hbm, out_hbm, new_ref, synced_ref, out_ref, sems, *, take):
    blocks, rows, depth = out_ref.shape
    loads, stores = [], []
    for i in range(rows // take):
        at = pl.ds(i * take, take)
        loads.append(
            (
                pltpu.make_async_copy(new_hbm.at[at], new_ref.at[at], sems.at[3 * i]),
                pltpu.make_async_copy(synced_hbm.at[at], synced_ref.at[at], sems.at[3 * i + 1]),
            )
        )
        stores.append(pltpu.make_async_copy(out_ref.at[:, at], out_hbm.at[:, at], sems.at[3 * i + 2]))
        loads[i][0].start()
        loads[i][1].start()
    for i, pair in enumerate(loads):
        pair[0].wait()
        pair[1].wait()
        at = slice(i * take, (i + 1) * take)
        for b in range(blocks):
            columns = slice(b * depth, (b + 1) * depth)
            out_ref[b, at] = (new_ref[at, columns] - synced_ref[at, columns]).astype(jnp.bfloat16)
        stores[i].start()
    for store in stores:
        store.wait()


def local_change(new_weight, synced_weight, blocks):
    rows, features = new_weight.shape
    take = divisor(rows, 24, 8)
    hbm = pl.BlockSpec(memory_space=pltpu.HBM)
    cut = (blocks, rows, features // blocks)
    return pl.pallas_call(
        functools.partial(change_kernel, take=take),
        out_shape=jax.ShapeDtypeStruct(cut, jnp.bfloat16),
        in_specs=[hbm] * 2,
        out_specs=hbm,
        scratch_shapes=[
            pltpu.VMEM((rows, features), jnp.float32),
            pltpu.VMEM((rows, features), jnp.float32),
            pltpu.VMEM(cut, jnp.bfloat16),
            pltpu.SemaphoreType.DMA((3 * (rows // take),)),
        ],
        compiler_params=limit(24),
        name="local_change",
    )(*held(pltpu.HBM, new_weight, synced_weight))


def fetch_kernel(own_hbm, other_hbm, own_ref, other_ref, sems):
    blocks = own_ref.shape[0]
    part = pl.ds(lax.axis_index("dp") * blocks, blocks)
    loads = [
        pltpu.make_async_copy(own_hbm.at[part], own_ref, sems.at[0]),
        pltpu.make_async_copy(other_hbm.at[part], other_ref, sems.at[1]),
    ]
    for load in loads:
        load.start()
    for load in loads:
        load.wait()


def fetch(own, other, blocks):
    cut = (blocks, *own.shape[1:])
    return pl.pallas_call(
        fetch_kernel,
        out_shape=[pltpu.VMEM(cut, own.dtype)] * 2,
        in_specs=[pl.BlockSpec(memory_space=pltpu.HBM)] * 2,
        out_specs=[pl.BlockSpec(memory_space=pltpu.VMEM)] * 2,
        scratch_shapes=[pltpu.SemaphoreType.DMA((2,))],
        compiler_params=limit(8),
        name="fetch",
    )(*held(pltpu.HBM, own, other))


def project_kernel(*refs, parts):
    gathered = refs[:parts]
    own_ref, other_ref, own_change_ref, other_change_ref = refs[parts : parts + 4]
    out_ref, rows_ref, sums_ref = refs[parts + 4 :]
    owners, steps, _ = out_ref.shape
    blocks, _, depth = own_ref.shape
    device = lax.axis_index("tensor")
    places = (device, device ^ 1)
    group = lax.axis_index("dp")

    pieces = []
    for part in gathered:
        for k in range(part.shape[0]):
            pieces.append(part[k].astype(jnp.float32))
    rows_ref[...] = jnp.concatenate(pieces, axis=0).astype(jnp.bfloat16)

    for source, ref in enumerate((own_ref, other_ref)):
        rows = rows_ref[:, pl.ds(pl.multiple_of(places[source] * depth, depth), depth)]
        for b in range(blocks):
            value = dot(ref[b], rows, NT)
            if source == 0:
                sums_ref[b] = value
            else:
                sums_ref[b] += value
    for source, ref in enumerate((own_change_ref, other_change_ref)):
        value = dot(ref[0], rows_ref[:, :depth], NT)
        for b in range(1, blocks):
            value += dot(ref[b], rows_ref[:, b * depth : (b + 1) * depth], NT)
        sums_ref[places[source]] += value
    sums = jnp.concatenate([sums_ref[b] for b in range(blocks)], axis=0).T
    each = owners // parts
    for k in range(owners):
        owner = (group ^ (k // each)) * each + k % each if parts > 1 else k
        out_ref[owner] = sums[k * steps : (k + 1) * steps]


def project(gathered, weights, owners, steps):
    blocks, width, depth = weights[0].shape
    take = owners if len(gathered) > 1 else divisor(owners, MOST, 1)
    several = owners > take
    whole = pl.BlockSpec(memory_space=pltpu.VMEM)
    cut = lambda s: pl.BlockSpec((take, *s[1:]), lambda i: (i, 0, 0)) if several else whole
    out = jax.ShapeDtypeStruct((owners, steps, blocks * width), jnp.float32)
    return pl.pallas_call(
        functools.partial(project_kernel, parts=len(gathered)),
        out_shape=out,
        grid=(owners // take,),
        in_specs=[*[cut(g.shape) for g in gathered], *[whole] * 4],
        out_specs=cut(out.shape),
        scratch_shapes=[
            pltpu.VMEM((take * steps, blocks * depth), jnp.bfloat16),
            pltpu.VMEM((blocks, width, take * steps), jnp.float32),
        ],
        compiler_params=limit(24 if not several else 40),
        name="project",
    )(
        *(gathered if several else held(pltpu.VMEM, *gathered)),
        *held(pltpu.VMEM, *weights),
    )


def norm_kernel(partial_ref, gain_ref, out_ref, sums_ref, *, groups):
    owners, _, columns = partial_ref.shape
    count = out_ref.shape[0]
    chips = owners // groups // count
    for r in range(count):
        for d in range(groups):
            value = partial_ref[d * chips * count + r]
            for z in range(1, chips):
                value += partial_ref[(d * chips + z) * count + r]
            sums_ref[:, d * columns : (d + 1) * columns] = value
        projected = sums_ref[...]
        mean_square = jnp.mean(projected * projected, axis=1, keepdims=True)
        out_ref[r] = (projected * lax.rsqrt(mean_square + 1e-06) * gain_ref[...]).astype(jnp.bfloat16)


def normalise(partial, gain, groups, count):
    steps, columns = partial.shape[1], partial.shape[2] * groups
    return pl.pallas_call(
        functools.partial(norm_kernel, groups=groups),
        out_shape=jax.ShapeDtypeStruct((count, steps, columns), jnp.bfloat16),
        in_specs=[pl.BlockSpec(memory_space=pltpu.VMEM)] * 2,
        out_specs=pl.BlockSpec(memory_space=pltpu.VMEM),
        scratch_shapes=[pltpu.VMEM((steps, columns), jnp.float32)],
        compiler_params=limit(8),
        name="normalise",
    )(partial, gain.reshape(1, columns))


def body(
    new_weight,
    synced_weight,
    resident,
    gain,
    query,
    cache_keys,
    cache_values,
    new_keys,
    new_values,
    cache_lengths,
):
    groups, devices = lax.axis_size("dp"), lax.axis_size("tensor")
    chips = devices // CORES
    count, steps, features = query.shape

    def exchange(value, axis, size, hop):
        return lax.ppermute(value, axis, [(i, i ^ hop) for i in range(size)])

    stored = resident.reshape(groups * devices, -1, resident.shape[1])
    copies = attend(query, cache_keys, cache_values, new_keys, new_values, cache_lengths, chips)
    column = lax.all_to_all(
        copies.reshape(chips * count, steps, features),
        "tensor",
        split_axis=0,
        concat_axis=0,
        tiled=True,
        axis_index_groups=[[i * CORES + c for i in range(chips)] for c in range(CORES)],
    )
    change = local_change(new_weight, synced_weight, devices)
    other = exchange(stored, "tensor", devices, 1)
    column, later = lax.optimization_barrier((column, change))
    other_change = exchange(later, "tensor", devices, 1)
    if groups <= FEW and groups & (groups - 1) == 0:
        gathered = [column]
        for hop in range(1, groups):
            gathered.append(exchange(column, "dp", groups, hop))
    else:
        gathered = [lax.all_gather(column, "dp", axis=0, tiled=True)]
    near = fetch(stored, other, devices)
    partial = project(gathered, [*near, change, other_change], groups * chips * count, steps)
    summed = lax.all_to_all(
        partial,
        ("dp", "tensor"),
        split_axis=0,
        concat_axis=0,
        tiled=True,
        axis_index_groups=[
            [g * devices + i * CORES + c for g in range(groups) for i in range(chips)] for c in range(CORES)
        ],
    )
    return normalise(summed, gain, groups, count)


def solution(mesh):
    in_specs = (
        P(("dp", "tensor"), None),
        P(("dp", "tensor"), None),
        P(None, "tensor"),
        P(),
        P(("dp", "tensor"), None, None),
        P(("dp", "tensor"), None, None),
        P(("dp", "tensor"), None, None),
        P(("dp", "tensor"), None, None),
        P(("dp", "tensor"), None, None),
        P(("dp", "tensor")),
    )
    out_specs = P(("dp", "tensor"), None, None)
    return jax.shard_map(body, mesh=mesh, in_specs=in_specs, out_specs=out_specs, check_vma=False)
```

time: 55.2 us -> 45 us (0.82)
  blocking collectives: 12.1 us -> 0 us
  starting transfers between devices: 8.65 us -> 14.1 us
  local copies, waits for them, and re-layouts: 3.14 us -> 0.02 us
  Pallas kernels: 16.9 us -> 15.8 us
  waiting for transfers between devices: 13.3 us -> 14.1 us
    all_to_all x1 -> x0, blocking collectives: 12.1 us -> none  [body(): lax.all_to_all(copies.reshape(chips * count, steps, features), 'tensor',...]
    all_to_all x0 -> x1, starting transfers between devices: none -> 5.87 us  [body(): lax.all_to_all(copies.reshape(chips * count, steps, features), 'tensor',...]
    unnamed x8 -> x2, local copies, waits for them, and re-layouts: 3.13 us -> 0.01 us
    all_to_all x0 -> x1, waiting for transfers between devices: none -> 1.98 us  [body(): lax.all_to_all(copies.reshape(chips * count, steps, features), 'tensor',...]
    ppermute x5, waiting for transfers between devices: 5.56 us -> 3.81 us  [exchange(): return lax.ppermute(value, axis, [(i, i ^ hop) for i in range(size)])]
    pallas_call x1, Pallas kernels: 6 us -> 4.51 us  [project(): pl.pallas_call(functools.partial(project_kernel, parts=len(gathered)), ou...]
    pallas_call x1 -> x2, Pallas kernels: 5.26 us -> 5.98 us  [the longest x1 3.35 us: attend(): pl.pallas_call(functools.partial(attend_kernel, width=width), out_shape=j...]
    ppermute x5, starting transfers between devices: 4.65 us -> 3.98 us  [exchange(): return lax.ppermute(value, axis, [(i, i ^ hop) for i in range(size)])]
  transfers between devices with their start and end apart: 6 -> 7, of which waited for: 3 -> 4; matrix products, arithmetic and copies ran while one was open for 0% -> 0% of each run, Pallas kernels for 9% -> 23%
where the time goes in v3:
time: 45 us; the launch traced here: 44.7 us
  Pallas kernels  15.8 us (35%)
  starting transfers between devices  14.1 us (31%)
  waiting for transfers between devices  14.1 us (31%)
  between operations  0.71 us (2%)
    all_to_all x1, waiting for transfers between devices, body(): lax.all_to_all(partial, ('dp', 'tensor'), split_axis=0, concat_axis=0, ti...  8.27 us
    all_to_all x1, starting transfers between devices, body(): lax.all_to_all(copies.reshape(chips * count, steps, features), 'tensor',...  5.87 us
    pallas_call x1, Pallas kernels, project(): pl.pallas_call(functools.partial(project_kernel, parts=len(gathered)), ou...  4.51 us
    pallas_call x1, Pallas kernels, local_change(): pl.pallas_call(functools.partial(change_kernel, take=take), out_shape=jax...  4.44 us
    all_to_all x1, starting transfers between devices, body(): lax.all_to_all(partial, ('dp', 'tensor'), split_axis=0, concat_axis=0, ti...  4.25 us
    ppermute x5, starting transfers between devices, exchange(): return lax.ppermute(value, axis, [(i, i ^ hop) for i in range(size)])  3.98 us
    ppermute x5, waiting for transfers between devices, exchange(): return lax.ppermute(value, axis, [(i, i ^ hop) for i in range(size)])  3.81 us
    pallas_call x1, Pallas kernels, attend(): pl.pallas_call(functools.partial(attend_kernel, width=width), out_shape=j...  3.35 us
  transfers between devices with their start and end apart: 7, of which 4 were waited for; matrix products, arithmetic and copies ran while one was open for 0% of the time, Pallas kernels for 23%

profile of v3, /device:TPU:0, one launch (start us, length us, event | category | flops | bytes accessed | tf_op | source)
XLA Modules:
  0.0 44.7 jit_solution(10521140330946039432)
XLA Ops:
  0.0 0.5 %collective-permute-start.3 = (bf16[32,168,1024]{2,1,0:T(8,128)(2,1)}, bf16[32,168,1024]{2,1,0:T(8,128)(2,1)}, u32[]{:S(2)}, u32[]{:S(2)}) collective-permute-start(bf16[32,168,1024]{2,1,0:T(8,128)(2,1)} %bitcast.2), channel_id=1, source_target_pairs={{0,1},{1,0},{2,3},{3,2},{4,5},{5,4},{6,7},{7,6},{8,9},{9,8},{10,11... | collective-permute-start | bytes 33030152 | tf_op jit(solution)/shard_map/ppermute | solution.py:338
  1.1 3.4 %attend.1 = bf16[4,1,2,8192]{3,2,1,0:T(2,128)(2,1)} custom-call(s32[1]{0:T(128)S(6)} %copy.11.lengths_ref, bf16[1,2,8192]{2,1,0:T(2,128)(2,1)} %query_hbm.1, bf16[1,768,1024]{2,1,0:T(8,128)(2,1)} %keys_hbm.1, bf16[1,768,1024]{2,1,0:T(8,128)(2,1)} %values_hbm.1, bf16[1,2,1024]{2,1,0:T(2,128)(2,1)} %new_keys_hbm.1, bf16[1,2,1024]{2,1,0:T(2,128)(2,1)} %new_values_hbm.1), custom_call_target="tpu_custom_call" | custom-call | tf_op jit(solution)/shard_map/attend/pallas_call | solution.py:142
  4.5 5.9 %all-to-all-start = ((bf16[4,2,8192]{2,1,0:T(2,128)(2,1)}), bf16[4,2,8192]{2,1,0:T(2,128)(2,1)S(1)}, u32[]{:S(2)}, u32[]{:S(2)}) async-start(bf16[4,2,8192]{2,1,0:T(2,128)(2,1)} %bitcast), calls=%async_computation | async-start | bytes 262144 | tf_op jit(solution)/shard_map/all_to_all | solution.py:342
  10.4 4.4 %local_change.1.refs_6_ = bf16[8,168,1024]{2,1,0:T(8,128)(2,1)S(1)} custom-call(f32[168,8192]{1,0:T(8,128)} %new_hbm.1, f32[168,8192]{1,0:T(8,128)} %synced_hbm.1), custom_call_target="tpu_custom_call" | custom-call | tf_op jit(solution)/shard_map/local_change/pallas_call | solution.py:190
  14.8 2.0 %all-to-all-done.refs_0_ = bf16[4,2,8192]{2,1,0:T(2,128)(2,1)S(1)} async-done(((bf16[4,2,8192]{2,1,0:T(2,128)(2,1)}), bf16[4,2,8192]{2,1,0:T(2,128)(2,1)S(1)}, u32[]{:S(2)}, u32[]{:S(2)}) %all-to-all-start) | async-done | bytes 131104 | tf_op jit(solution)/shard_map/all_to_all | solution.py:342
  16.8 0.0 collective-permute-start.4
  16.8 1.5 %collective-permute-start = (bf16[4,2,8192]{2,1,0:T(2,128)(2,1)S(1)}, bf16[4,2,8192]{2,1,0:T(2,128)(2,1)S(1)}, u32[]{:S(2)}, u32[]{:S(2)}) collective-permute-start(bf16[4,2,8192]{2,1,0:T(2,128)(2,1)S(1)} %all-to-all-done.refs_0_), channel_id=1, source_target_pairs={{0,8},{8,0},{16,24},{24,16},{1,9},{9,1},{17,25},{25,17},{2,10},{10... | collective-permute-start | bytes 393224 | tf_op jit(solution)/shard_map/ppermute | solution.py:338
  18.3 1.5 %collective-permute-start.1 = (bf16[4,2,8192]{2,1,0:T(2,128)(2,1)S(1)}, bf16[4,2,8192]{2,1,0:T(2,128)(2,1)S(1)}, u32[]{:S(2)}, u32[]{:S(2)}) collective-permute-start(bf16[4,2,8192]{2,1,0:T(2,128)(2,1)S(1)} %all-to-all-done.refs_0_), channel_id=1, source_target_pairs={{0,16},{8,24},{16,0},{24,8},{1,17},{9,25},{17,1},{25,9},{2,18},{10... | collective-permute-start | bytes 393224 | tf_op jit(solution)/shard_map/ppermute | solution.py:338
  19.8 0.5 %collective-permute-start.2 = (bf16[4,2,8192]{2,1,0:T(2,128)(2,1)S(1)}, bf16[4,2,8192]{2,1,0:T(2,128)(2,1)S(1)}, u32[]{:S(2)}, u32[]{:S(2)}) collective-permute-start(bf16[4,2,8192]{2,1,0:T(2,128)(2,1)S(1)} %all-to-all-done.refs_0_), channel_id=1, source_target_pairs={{0,24},{8,16},{16,8},{24,0},{1,25},{9,17},{17,9},{25,1},{2,26},{10... | collective-permute-start | bytes 393224 | tf_op jit(solution)/shard_map/ppermute | solution.py:338
  20.3 0.0 collective-permute-done.3.other_hbm
  20.3 2.6 %fetch.1 = (bf16[8,168,1024]{2,1,0:T(8,128)(2,1)S(1)}, bf16[8,168,1024]{2,1,0:T(8,128)(2,1)S(1)}) custom-call(bf16[32,168,1024]{2,1,0:T(8,128)(2,1)} %bitcast.3, bf16[32,168,1024]{2,1,0:T(8,128)(2,1)} %collective-permute-done.3.other_hbm), custom_call_target="tpu_custom_call" | custom-call | tf_op jit(solution)/shard_map/fetch/pallas_call | solution.py:221
  22.9 0.2 collective-permute-done.refs_1_
  23.1 3.6 %collective-permute-done.1.refs_2_ = bf16[4,2,8192]{2,1,0:T(2,128)(2,1)S(1)} collective-permute-done((bf16[4,2,8192]{2,1,0:T(2,128)(2,1)S(1)}, bf16[4,2,8192]{2,1,0:T(2,128)(2,1)S(1)}, u32[]{:S(2)}, u32[]{:S(2)}) %collective-permute-start.1) | collective-permute-done | bytes 131104 | tf_op jit(solution)/shard_map/ppermute | solution.py:338
  26.7 0.0 collective-permute-done.2.refs_3_
  26.7 0.0 collective-permute-done.4.refs_7_
  26.7 0.0 copy-start
  26.7 4.5 %project.1 = f32[16,2,1344]{2,1,0:T(2,128)} custom-call(bf16[4,2,8192]{2,1,0:T(2,128)(2,1)S(1)} %all-to-all-done.refs_0_, bf16[4,2,8192]{2,1,0:T(2,128)(2,1)S(1)} %collective-permute-done.refs_1_, bf16[4,2,8192]{2,1,0:T(2,128)(2,1)S(1)} %collective-permute-done.1.refs_2_, bf16[4,2,8192]{2,1,0:T(2,128)(2,1)S(1)} %collective-permute-done.2.refs_3_, ...), custom_call_target="tpu_custom_call" | custom-call | tf_op jit(solution)/shard_map/project/pallas_call | solution.py:275
  31.3 4.3 %all-to-all-start.1 = ((f32[16,2,1344]{2,1,0:T(2,128)}), f32[16,2,1344]{2,1,0:T(2,128)S(1)}, u32[]{:S(2)}, u32[]{:S(2)}) async-start(f32[16,2,1344]{2,1,0:T(2,128)} %project.1), calls=%async_computation.1 | async-start | bytes 360448 | tf_op jit(solution)/shard_map/all_to_all | solution.py:362
  35.5 0.0 copy-done
  35.6 8.3 %all-to-all-done.1.partial_ref = f32[16,2,1344]{2,1,0:T(2,128)S(1)} async-done(((f32[16,2,1344]{2,1,0:T(2,128)}), f32[16,2,1344]{2,1,0:T(2,128)S(1)}, u32[]{:S(2)}, u32[]{:S(2)}) %all-to-all-start.1) | async-done | bytes 172064 | tf_op jit(solution)/shard_map/all_to_all | solution.py:362
  43.8 0.8 %normalise.1 = bf16[1,2,5376]{2,1,0:T(2,128)(2,1)} custom-call(f32[16,2,1344]{2,1,0:T(2,128)S(1)} %all-to-all-done.1.partial_ref, f32[1,5376]{1,0:T(1,128)S(1)} %reshape.11.gain_ref), custom_call_target="tpu_custom_call" | custom-call | tf_op jit(solution)/shard_map/normalise/pallas_call | solution.py:310
  (1 shorter events, 0.0 us)
Async XLA Ops:
  0.0 20.3 %collective-permute-start.3 = (bf16[32,168,1024]{2,1,0:T(8,128)(2,1)}, bf16[32,168,1024]{2,1,0:T(8,128)(2,1)}, u32[]{:S(2)}, u32[]{:S(2)}) collective-permute-start(bf16[32,168,1024]{2,1,0:T(8,128)(2,1)} %bitcast.2), channel_id=1, source_target_pairs={{0,1},{1,0},{2,3},{3,2},{4,5},{5,4},{6,7},{7,6},{8,9},{9,8},{10,11... | collective-permute-start | bytes 33030152 | tf_op jit(solution)/shard_map/ppermute | solution.py:338
  4.5 12.3 %all-to-all-start = ((bf16[4,2,8192]{2,1,0:T(2,128)(2,1)}), bf16[4,2,8192]{2,1,0:T(2,128)(2,1)S(1)}, u32[]{:S(2)}, u32[]{:S(2)}) async-start(bf16[4,2,8192]{2,1,0:T(2,128)(2,1)} %bitcast), calls=%async_computation | async-start | bytes 262144 | tf_op jit(solution)/shard_map/all_to_all | solution.py:342
  16.8 9.9 %collective-permute-start.4 = (bf16[8,168,1024]{2,1,0:T(8,128)(2,1)S(1)}, bf16[8,168,1024]{2,1,0:T(8,128)(2,1)S(1)}, u32[]{:S(2)}, u32[]{:S(2)}) collective-permute-start(bf16[8,168,1024]{2,1,0:T(8,128)(2,1)S(1)} %local_change.1.refs_6_), channel_id=1, source_target_pairs={{0,1},{1,0},{2,3},{3,2},{4,5},{5,4},{6,7},{7,6},{8,9},{9,8},{10,11... | collective-permute-start | bytes 8257544 | tf_op jit(solution)/shard_map/ppermute | solution.py:338
  16.8 6.3 %collective-permute-start = (bf16[4,2,8192]{2,1,0:T(2,128)(2,1)S(1)}, bf16[4,2,8192]{2,1,0:T(2,128)(2,1)S(1)}, u32[]{:S(2)}, u32[]{:S(2)}) collective-permute-start(bf16[4,2,8192]{2,1,0:T(2,128)(2,1)S(1)} %all-to-all-done.refs_0_), channel_id=1, source_target_pairs={{0,8},{8,0},{16,24},{24,16},{1,9},{9,1},{17,25},{25,17},{2,10},{10... | collective-permute-start | bytes 393224 | tf_op jit(solution)/shard_map/ppermute | solution.py:338
  18.3 8.4 %collective-permute-start.1 = (bf16[4,2,8192]{2,1,0:T(2,128)(2,1)S(1)}, bf16[4,2,8192]{2,1,0:T(2,128)(2,1)S(1)}, u32[]{:S(2)}, u32[]{:S(2)}) collective-permute-start(bf16[4,2,8192]{2,1,0:T(2,128)(2,1)S(1)} %all-to-all-done.refs_0_), channel_id=1, source_target_pairs={{0,16},{8,24},{16,0},{24,8},{1,17},{9,25},{17,1},{25,9},{2,18},{10... | collective-permute-start | bytes 393224 | tf_op jit(solution)/shard_map/ppermute | solution.py:338
  19.8 6.9 %collective-permute-start.2 = (bf16[4,2,8192]{2,1,0:T(2,128)(2,1)S(1)}, bf16[4,2,8192]{2,1,0:T(2,128)(2,1)S(1)}, u32[]{:S(2)}, u32[]{:S(2)}) collective-permute-start(bf16[4,2,8192]{2,1,0:T(2,128)(2,1)S(1)} %all-to-all-done.refs_0_), channel_id=1, source_target_pairs={{0,24},{8,16},{16,8},{24,0},{1,25},{9,17},{17,9},{25,1},{2,26},{10... | collective-permute-start | bytes 393224 | tf_op jit(solution)/shard_map/ppermute | solution.py:338
  26.7 8.8 %copy-start = (f32[5376]{0:T(1024)S(1)}, f32[5376]{0:T(1024)}, u32[]{:S(2)}) copy-start(f32[5376]{0:T(1024)} %param.13) | copy-start | bytes 64516
  31.3 12.6 %all-to-all-start.1 = ((f32[16,2,1344]{2,1,0:T(2,128)}), f32[16,2,1344]{2,1,0:T(2,128)S(1)}, u32[]{:S(2)}, u32[]{:S(2)}) async-start(f32[16,2,1344]{2,1,0:T(2,128)} %project.1), calls=%async_computation.1 | async-start | bytes 360448 | tf_op jit(solution)/shard_map/all_to_all | solution.py:362

commit v4 on v3

--- a/solution.py
+++ b/solution.py
@@ -40,7 +40,9 @@
     values_hbm,
     new_keys_hbm,
     new_values_hbm,
-    out_hbm,
+    resident_hbm,
+    out_ref,
+    near_ref,
     query_ref,
     keys_ref,
     values_ref,
@@ -48,7 +50,6 @@
     new_values_ref,
     past_ref,
     own_ref,
-    out_ref,
     sems,
     *,
     width,
@@ -61,6 +62,8 @@
     block_rows = grouping * steps
     rows = heads * block_rows
     factor = HD ** (-0.5)
+    blocks = near_ref.shape[0]
+    near = pltpu.make_async_copy(resident_hbm.at[pl.ds(lax.axis_index("dp") * blocks, blocks)], near_ref, sems.at[5])
     for row in range(count):
         pairs = [
             (query_hbm, query_ref),
@@ -72,6 +75,8 @@
         loads = [pltpu.make_async_copy(p[0].at[row], p[1], sems.at[i]) for i, p in enumerate(pairs)]
         for load in loads:
             load.start()
+        if row == 0:
+            near.start()
 
         padding = jnp.zeros((8 - steps % 8, kv_features), jnp.float32)
         loads[0].wait()
@@ -121,18 +126,11 @@
                     head = (band * heads + k) * grouping + g
                     piece = k * block_rows + g * steps
                     value = attended[piece : piece + steps, k * HD : (k + 1) * HD]
-                    out_ref[:, head * HD : (head + 1) * HD] = value.astype(jnp.bfloat16)
-        stores = [
-            pltpu.make_async_copy(out_ref, out_hbm.at[copy, row], sems.at[5 + copy])
-            for copy in range(out_hbm.shape[0])
-        ]
-        for store in stores:
-            store.start()
-        for store in stores:
-            store.wait()
-
-
-def attend(query, cache_keys, cache_values, new_keys, new_values, cache_lengths, copies):
+                    out_ref[row, :, head * HD : (head + 1) * HD] = value.astype(jnp.bfloat16)
+    near.wait()
+
+
+def attend(query, cache_keys, cache_values, new_keys, new_values, cache_lengths, stored, blocks):
     _, steps, features = query.shape
     slots, kv_features = cache_keys.shape[1:]
     width = HD * 2 if kv_features % (HD * 2) == 0 else HD
@@ -141,33 +139,51 @@
     operands = held(pltpu.HBM, query, cache_keys, cache_values, new_keys, new_values)
     return pl.pallas_call(
         functools.partial(attend_kernel, width=width),
-        out_shape=jax.ShapeDtypeStruct((copies, *query.shape), query.dtype),
-        in_specs=[pl.BlockSpec(memory_space=pltpu.SMEM), *[hbm] * len(operands)],
-        out_specs=hbm,
+        out_shape=[pltpu.VMEM(query.shape, query.dtype), pltpu.VMEM((blocks, *stored.shape[1:]), stored.dtype)],
+        in_specs=[pl.BlockSpec(memory_space=pltpu.SMEM), *[hbm] * (len(operands) + 1)],
+        out_specs=[pl.BlockSpec(memory_space=pltpu.VMEM)] * 2,
         scratch_shapes=[
             *[pltpu.VMEM(o.shape[1:], o.dtype) for o in operands],
             pltpu.VMEM((lines, slots), jnp.float32),
             pltpu.VMEM((lines, 8 * (steps // 8 + 1)), jnp.float32),
-            pltpu.VMEM(query.shape[1:], query.dtype),
-            pltpu.SemaphoreType.DMA((5 + copies,)),
+            pltpu.SemaphoreType.DMA((6,)),
         ],
         compiler_params=limit(16),
         name="attend",
-    )(cache_lengths, *operands)
-
-
-def change_kernel(new_hbm, synced_hbm, out_hbm, new_ref, synced_ref, out_ref, sems, *, take):
+    )(cache_lengths, *operands, *held(pltpu.HBM, stored))
+
+
+def join_kernel(*refs):
+    *part_refs, out_ref = refs
+    count = part_refs[0].shape[0]
+    for i, ref in enumerate(part_refs):
+        out_ref[i * count : (i + 1) * count] = ref[...]
+
+
+def join(parts):
+    whole = pl.BlockSpec(memory_space=pltpu.VMEM)
+    count = parts[0].shape[0]
+    return pl.pallas_call(
+        join_kernel,
+        out_shape=pltpu.VMEM((count * len(parts), *parts[0].shape[1:]), parts[0].dtype),
+        in_specs=[whole] * len(parts),
+        out_specs=whole,
+        compiler_params=limit(4),
+        name="join",
+    )(*held(pltpu.VMEM, *parts))
+
+
+def change_kernel(new_hbm, synced_hbm, out_ref, new_ref, synced_ref, sems, *, first, take):
     blocks, rows, depth = out_ref.shape
-    loads, stores = [], []
+    loads = []
     for i in range(rows // take):
-        at = pl.ds(i * take, take)
+        at, near = pl.ds(first + i * take, take), pl.ds(i * take, take)
         loads.append(
             (
-                pltpu.make_async_copy(new_hbm.at[at], new_ref.at[at], sems.at[3 * i]),
-                pltpu.make_async_copy(synced_hbm.at[at], synced_ref.at[at], sems.at[3 * i + 1]),
+                pltpu.make_async_copy(new_hbm.at[at], new_ref.at[near], sems.at[2 * i]),
+                pltpu.make_async_copy(synced_hbm.at[at], synced_ref.at[near], sems.at[2 * i + 1]),
             )
         )
-        stores.append(pltpu.make_async_copy(out_ref.at[:, at], out_hbm.at[:, at], sems.at[3 * i + 2]))
         loads[i][0].start()
         loads[i][1].start()
     for i, pair in enumerate(loads):
@@ -177,67 +193,33 @@
         for b in range(blocks):
             columns = slice(b * depth, (b + 1) * depth)
             out_ref[b, at] = (new_ref[at, columns] - synced_ref[at, columns]).astype(jnp.bfloat16)
-        stores[i].start()
-    for store in stores:
-        store.wait()
-
-
-def local_change(new_weight, synced_weight, blocks):
-    rows, features = new_weight.shape
-    take = divisor(rows, 24, 8)
-    hbm = pl.BlockSpec(memory_space=pltpu.HBM)
-    cut = (blocks, rows, features // blocks)
-    return pl.pallas_call(
-        functools.partial(change_kernel, take=take),
-        out_shape=jax.ShapeDtypeStruct(cut, jnp.bfloat16),
-        in_specs=[hbm] * 2,
-        out_specs=hbm,
+
+
+def local_change(new_weight, synced_weight, blocks, first, rows, take):
+    features = new_weight.shape[1]
+    return pl.pallas_call(
+        functools.partial(change_kernel, first=first, take=take),
+        out_shape=pltpu.VMEM((blocks, rows, features // blocks), jnp.bfloat16),
+        in_specs=[pl.BlockSpec(memory_space=pltpu.HBM)] * 2,
+        out_specs=pl.BlockSpec(memory_space=pltpu.VMEM),
         scratch_shapes=[
             pltpu.VMEM((rows, features), jnp.float32),
             pltpu.VMEM((rows, features), jnp.float32),
-            pltpu.VMEM(cut, jnp.bfloat16),
-            pltpu.SemaphoreType.DMA((3 * (rows // take),)),
+            pltpu.SemaphoreType.DMA((2 * (rows // take),)),
         ],
-        compiler_params=limit(24),
+        compiler_params=limit(14),
         name="local_change",
     )(*held(pltpu.HBM, new_weight, synced_weight))
 
 
-def fetch_kernel(own_hbm, other_hbm, own_ref, other_ref, sems):
-    blocks = own_ref.shape[0]
-    part = pl.ds(lax.axis_index("dp") * blocks, blocks)
-    loads = [
-        pltpu.make_async_copy(own_hbm.at[part], own_ref, sems.at[0]),
-        pltpu.make_async_copy(other_hbm.at[part], other_ref, sems.at[1]),
-    ]
-    for load in loads:
-        load.start()
-    for load in loads:
-        load.wait()
-
-
-def fetch(own, other, blocks):
-    cut = (blocks, *own.shape[1:])
-    return pl.pallas_call(
-        fetch_kernel,
-        out_shape=[pltpu.VMEM(cut, own.dtype)] * 2,
-        in_specs=[pl.BlockSpec(memory_space=pltpu.HBM)] * 2,
-        out_specs=[pl.BlockSpec(memory_space=pltpu.VMEM)] * 2,
-        scratch_shapes=[pltpu.SemaphoreType.DMA((2,))],
-        compiler_params=limit(8),
-        name="fetch",
-    )(*held(pltpu.HBM, own, other))
-
-
-def project_kernel(*refs, parts):
-    gathered = refs[:parts]
-    own_ref, other_ref, own_change_ref, other_change_ref = refs[parts : parts + 4]
-    out_ref, rows_ref, sums_ref = refs[parts + 4 :]
+def project_kernel(*refs, parts, cuts):
+    gathered, refs = refs[:parts], refs[parts:]
+    changes, (own_ref, other_ref, out_ref, rows_ref, sums_ref) = refs[: 2 * cuts], refs[2 * cuts :]
     owners, steps, _ = out_ref.shape
     blocks, _, depth = own_ref.shape
     device = lax.axis_index("tensor")
     places = (device, device ^ 1)
-    group = lax.axis_index("dp")
+    group, chip = lax.axis_index("dp"), device // CORES
 
     pieces = []
     for part in gathered:
@@ -245,6 +227,12 @@
             pieces.append(part[k].astype(jnp.float32))
     rows_ref[...] = jnp.concatenate(pieces, axis=0).astype(jnp.bfloat16)
 
+    deltas = []
+    for ref in changes:
+        value = dot(ref[0], rows_ref[:, :depth], NT)
+        for b in range(1, blocks):
+            value += dot(ref[b], rows_ref[:, b * depth : (b + 1) * depth], NT)
+        deltas.append(value)
     for source, ref in enumerate((own_ref, other_ref)):
         rows = rows_ref[:, pl.ds(pl.multiple_of(places[source] * depth, depth), depth)]
         for b in range(blocks):
@@ -253,40 +241,49 @@
                 sums_ref[b] = value
             else:
                 sums_ref[b] += value
-    for source, ref in enumerate((own_change_ref, other_change_ref)):
-        value = dot(ref[0], rows_ref[:, :depth], NT)
-        for b in range(1, blocks):
-            value += dot(ref[b], rows_ref[:, b * depth : (b + 1) * depth], NT)
-        sums_ref[places[source]] += value
+    for source in range(2):
+        first = 0
+        for value in deltas[source * cuts : (source + 1) * cuts]:
+            sums_ref[places[source], first : first + value.shape[0]] += value
+            first += value.shape[0]
     sums = jnp.concatenate([sums_ref[b] for b in range(blocks)], axis=0).T
     each = owners // parts
     for k in range(owners):
-        owner = (group ^ (k // each)) * each + k % each if parts > 1 else k
+        owner = k
+        if parts > 1:
+            chips = device_count() // CORES
+            count = each // chips
+            hop, r = k % each // count, k % count
+            owner = ((group ^ (k // each)) * chips + (chip ^ hop)) * count + r
         out_ref[owner] = sums[k * steps : (k + 1) * steps]
 
 
-def project(gathered, weights, owners, steps):
-    blocks, width, depth = weights[0].shape
+def device_count():
+    return lax.axis_size("tensor")
+
+
+def project(gathered, changes, own, other, owners, steps):
+    blocks, width, depth = own.shape
     take = owners if len(gathered) > 1 else divisor(owners, MOST, 1)
     several = owners > take
     whole = pl.BlockSpec(memory_space=pltpu.VMEM)
     cut = lambda s: pl.BlockSpec((take, *s[1:]), lambda i: (i, 0, 0)) if several else whole
     out = jax.ShapeDtypeStruct((owners, steps, blocks * width), jnp.float32)
     return pl.pallas_call(
-        functools.partial(project_kernel, parts=len(gathered)),
+        functools.partial(project_kernel, parts=len(gathered), cuts=len(changes) // 2),
         out_shape=out,
         grid=(owners // take,),
-        in_specs=[*[cut(g.shape) for g in gathered], *[whole] * 4],
+        in_specs=[*[cut(g.shape) for g in gathered], *[whole] * (len(changes) + 2)],
         out_specs=cut(out.shape),
         scratch_shapes=[
             pltpu.VMEM((take * steps, blocks * depth), jnp.bfloat16),
             pltpu.VMEM((blocks, width, take * steps), jnp.float32),
         ],
-        compiler_params=limit(24 if not several else 40),
+        compiler_params=limit(16 if not several else 40),
         name="project",
     )(
         *(gathered if several else held(pltpu.VMEM, *gathered)),
-        *held(pltpu.VMEM, *weights),
+        *held(pltpu.VMEM, *changes, own, other),
     )
 
 
@@ -332,33 +329,41 @@
 ):
     groups, devices = lax.axis_size("dp"), lax.axis_size("tensor")
     chips = devices // CORES
-    count, steps, features = query.shape
-
-    def exchange(value, axis, size, hop):
-        return lax.ppermute(value, axis, [(i, i ^ hop) for i in range(size)])
-
-    stored = resident.reshape(groups * devices, -1, resident.shape[1])
-    copies = attend(query, cache_keys, cache_values, new_keys, new_values, cache_lengths, chips)
-    column = lax.all_to_all(
-        copies.reshape(chips * count, steps, features),
-        "tensor",
-        split_axis=0,
-        concat_axis=0,
-        tiled=True,
-        axis_index_groups=[[i * CORES + c for i in range(chips)] for c in range(CORES)],
-    )
-    change = local_change(new_weight, synced_weight, devices)
-    other = exchange(stored, "tensor", devices, 1)
-    column, later = lax.optimization_barrier((column, change))
-    other_change = exchange(later, "tensor", devices, 1)
-    if groups <= FEW and groups & (groups - 1) == 0:
+    count, steps, _ = query.shape
+
+    def exchange(value, axis, size, unit, hop):
+        return lax.ppermute(value, axis, [(i, (i // unit ^ hop) * unit + i % unit) for i in range(size)])
+
+    def fits(size):
+        return size <= FEW and size & (size - 1) == 0
+
+    rows = new_weight.shape[0]
+    take = divisor(rows, 24, 8)
+    early = (rows // take - rows // take // 3) * take
+    stored = resident.reshape(groups * devices, rows, resident.shape[1])
+    attended, own_rows = attend(query, cache_keys, cache_values, new_keys, new_values, cache_lengths, stored, devices)
+    other_rows = exchange(own_rows, "tensor", devices, 1, 1)
+    near = fits(chips) and fits(groups)
+    if near:
+        column = [attended]
+        for hop in range(1, chips):
+            column.append(exchange(attended, "tensor", devices, CORES, hop))
+        column = join(column)
+    else:
+        alike = [[i * CORES + c for i in range(chips)] for c in range(CORES)]
+        column = lax.all_gather(attended, "tensor", axis=0, tiled=True, axis_index_groups=alike)
+    if near:
         gathered = [column]
         for hop in range(1, groups):
-            gathered.append(exchange(column, "dp", groups, hop))
+            gathered.append(exchange(column, "dp", groups, 1, hop))
     else:
         gathered = [lax.all_gather(column, "dp", axis=0, tiled=True)]
-    near = fetch(stored, other, devices)
-    partial = project(gathered, [*near, change, other_change], groups * chips * count, steps)
+    own, swapped = [], []
+    for first, size in ((0, early), (early, rows - early)):
+        if size:
+            own.append(local_change(new_weight, synced_weight, devices, first, size, take))
+            swapped.append(exchange(own[-1], "tensor", devices, 1, 1))
+    partial = project(gathered, own + swapped, own_rows, other_rows, groups * chips * count, steps)
     summed = lax.all_to_all(
         partial,
         ("dp", "tensor"),

time: 45 us -> 52 us (1.16)
  starting transfers between devices: 14.1 us -> 22.3 us
  Pallas kernels: 15.8 us -> 13.1 us
  waiting for transfers between devices: 14.1 us -> 15.5 us
    ppermute x5 -> x9, starting transfers between devices: 3.98 us -> 15.3 us  [exchange(): lax.ppermute(value, axis, [(i, (i // unit ^ hop) * unit + i % unit) for i...]
    all_to_all x1 -> x0, starting transfers between devices: 5.87 us -> none  [body(): lax.all_to_all(copies.reshape(chips * count, steps, features), 'tensor',...]
    ppermute x5 -> x9, waiting for transfers between devices: 3.81 us -> 7.75 us  [exchange(): lax.ppermute(value, axis, [(i, (i // unit ^ hop) * unit + i % unit) for i...]
    all_to_all x1, starting transfers between devices: 4.25 us -> 6.99 us  [body(): lax.all_to_all(partial, ('dp', 'tensor'), split_axis=0, concat_axis=0, ti...]
    pallas_call x4 -> x5, Pallas kernels: 14.9 us -> 12.3 us  [the longest x2 5.34 us: local_change(): pl.pallas_call(functools.partial(change_kernel, first=first, take=take),...]
    all_to_all x1 -> x0, waiting for transfers between devices: 1.98 us -> none  [body(): lax.all_to_all(copies.reshape(chips * count, steps, features), 'tensor',...]
  transfers between devices with their start and end apart: 7 -> 10, of which waited for: 4 -> 5; matrix products, arithmetic and copies ran while one was open for 0% -> 0% of each run, Pallas kernels for 23% -> 10%
where the time goes in v4:
time: 52 us; the launch traced here: 51.7 us
  starting transfers between devices  22.3 us (43%)
  waiting for transfers between devices  15.5 us (30%)
  Pallas kernels  13.1 us (25%)
  between operations  0.72 us (1%)
    ppermute x9, starting transfers between devices, exchange(): lax.ppermute(value, axis, [(i, (i // unit ^ hop) * unit + i % unit) for i...  15.3 us
    all_to_all x1, waiting for transfers between devices, body(): lax.all_to_all(partial, ('dp', 'tensor'), split_axis=0, concat_axis=0, ti...  7.78 us
    ppermute x9, waiting for transfers between devices, exchange(): lax.ppermute(value, axis, [(i, (i // unit ^ hop) * unit + i % unit) for i...  7.75 us
    all_to_all x1, starting transfers between devices, body(): lax.all_to_all(partial, ('dp', 'tensor'), split_axis=0, concat_axis=0, ti...  6.99 us
    pallas_call x2, Pallas kernels, local_change(): pl.pallas_call(functools.partial(change_kernel, first=first, take=take),...  5.34 us
    pallas_call x1, Pallas kernels, project(): pl.pallas_call(functools.partial(project_kernel, parts=len(gathered), cut...  4.13 us
    pallas_call x1, Pallas kernels, attend(): pl.pallas_call(functools.partial(attend_kernel, width=width), out_shape=[...  2.83 us
  transfers between devices with their start and end apart: 10, of which 5 were waited for; matrix products, arithmetic and copies ran while one was open for 0% of the time, Pallas kernels for 10%

profile of v4, /device:TPU:0, one launch (start us, length us, event | category | flops | bytes accessed | tf_op | source)
XLA Modules:
  0.0 51.7 jit_solution(14298398177578156230)
XLA Ops:
  0.7 2.8 %attend.1 = (bf16[1,2,8192]{2,1,0:T(2,128)(2,1)S(1)}, bf16[8,168,1024]{2,1,0:T(8,128)(2,1)S(1)}) custom-call(s32[1]{0:T(128)S(6)} %copy.11.lengths_ref, bf16[1,2,8192]{2,1,0:T(2,128)(2,1)} %query_hbm.1, bf16[1,768,1024]{2,1,0:T(8,128)(2,1)} %keys_hbm.1, bf16[1,768,1024]{2,1,0:T(8,128)(2,1)} %values_hbm.1, bf16[1,2,1024]{2,1,0:T(2,128)(2,1)} %new_keys_hbm.1, ...), custom_call_target="tpu_custom_call" | custom-call | tf_op jit(solution)/shard_map/attend/pallas_call | solution.py:140
  3.5 0.6 %collective-permute-start.8 = (bf16[8,168,1024]{2,1,0:T(8,128)(2,1)S(1)}, bf16[8,168,1024]{2,1,0:T(8,128)(2,1)S(1)}, u32[]{:S(2)}, u32[]{:S(2)}) collective-permute-start(bf16[8,168,1024]{2,1,0:T(8,128)(2,1)S(1)} %get-tuple-element.8.refs_8_), channel_id=1, source_target_pairs={{0,1},{1,0},{2,3},{3,2},{4,5},{5,4},{6,7},{7,6},{8,9},{9,8},{10,11... | collective-permute-start | bytes 8257544 | tf_op jit(solution)/shard_map/ppermute | solution.py:335
  4.1 3.4 %local_change.2.refs_4_ = bf16[8,120,1024]{2,1,0:T(8,128)(2,1)S(1)} custom-call(f32[168,8192]{1,0:T(8,128)} %new_hbm.3, f32[168,8192]{1,0:T(8,128)} %synced_hbm.3), custom_call_target="tpu_custom_call" | custom-call | tf_op jit(solution)/shard_map/local_change/pallas_call | solution.py:200
  7.5 0.1 collective-permute-start.6
  7.5 1.9 %local_change.3.refs_5_ = bf16[8,48,1024]{2,1,0:T(8,128)(2,1)S(1)} custom-call(f32[168,8192]{1,0:T(8,128)} %new_hbm.3, f32[168,8192]{1,0:T(8,128)} %synced_hbm.3), custom_call_target="tpu_custom_call" | custom-call | tf_op jit(solution)/shard_map/local_change/pallas_call | solution.py:200
  9.5 0.6 %collective-permute-start.7 = (bf16[8,48,1024]{2,1,0:T(8,128)(2,1)S(1)}, bf16[8,48,1024]{2,1,0:T(8,128)(2,1)S(1)}, u32[]{:S(2)}, u32[]{:S(2)}) collective-permute-start(bf16[8,48,1024]{2,1,0:T(8,128)(2,1)S(1)} %local_change.3.refs_5_), channel_id=1, source_target_pairs={{0,1},{1,0},{2,3},{3,2},{4,5},{5,4},{6,7},{7,6},{8,9},{9,8},{10,11... | collective-permute-start | bytes 2359304 | tf_op jit(solution)/shard_map/ppermute | solution.py:335
  10.0 2.6 %collective-permute-start = (bf16[1,2,8192]{2,1,0:T(2,128)(2,1)S(1)}, bf16[1,2,8192]{2,1,0:T(2,128)(2,1)S(1)}, u32[]{:S(2)}, u32[]{:S(2)}) collective-permute-start(bf16[1,2,8192]{2,1,0:T(2,128)(2,1)S(1)} %get-tuple-element.7.refs_0_), channel_id=1, source_target_pairs={{0,2},{1,3},{2,0},{3,1},{4,6},{5,7},{6,4},{7,5},{8,10},{9,11},{10,... | collective-permute-start | bytes 98312 | tf_op jit(solution)/shard_map/ppermute | solution.py:335
  12.7 2.6 %collective-permute-start.1 = (bf16[1,2,8192]{2,1,0:T(2,128)(2,1)S(1)}, bf16[1,2,8192]{2,1,0:T(2,128)(2,1)S(1)}, u32[]{:S(2)}, u32[]{:S(2)}) collective-permute-start(bf16[1,2,8192]{2,1,0:T(2,128)(2,1)S(1)} %get-tuple-element.7.refs_0_), channel_id=1, source_target_pairs={{0,4},{1,5},{2,6},{3,7},{4,0},{5,1},{6,2},{7,3},{8,12},{9,13},{10,... | collective-permute-start | bytes 98312 | tf_op jit(solution)/shard_map/ppermute | solution.py:335
  15.3 0.0 collective-permute-done.refs_1_
  15.3 3.3 %collective-permute-start.2 = (bf16[1,2,8192]{2,1,0:T(2,128)(2,1)S(1)}, bf16[1,2,8192]{2,1,0:T(2,128)(2,1)S(1)}, u32[]{:S(2)}, u32[]{:S(2)}) collective-permute-start(bf16[1,2,8192]{2,1,0:T(2,128)(2,1)S(1)} %get-tuple-element.7.refs_0_), channel_id=1, source_target_pairs={{0,6},{1,7},{2,4},{3,5},{4,2},{5,3},{6,0},{7,1},{8,14},{9,15},{10,... | collective-permute-start | bytes 98312 | tf_op jit(solution)/shard_map/ppermute | solution.py:335
  18.6 0.0 collective-permute-done.1.refs_2_
  18.6 2.4 %collective-permute-done.2.refs_3_ = bf16[1,2,8192]{2,1,0:T(2,128)(2,1)S(1)} collective-permute-done((bf16[1,2,8192]{2,1,0:T(2,128)(2,1)S(1)}, bf16[1,2,8192]{2,1,0:T(2,128)(2,1)S(1)}, u32[]{:S(2)}, u32[]{:S(2)}) %collective-permute-start.2) | collective-permute-done | bytes 32800 | tf_op jit(solution)/shard_map/ppermute | solution.py:335
  21.0 0.0 copy-start
  21.0 1.6 %collective-permute-start.3 = (bf16[4,2,8192]{2,1,0:T(2,128)(2,1)S(1)}, bf16[4,2,8192]{2,1,0:T(2,128)(2,1)S(1)}, u32[]{:S(2)}, u32[]{:S(2)}) collective-permute-start(bf16[4,2,8192]{2,1,0:T(2,128)(2,1)S(1)} %join.1.refs_0_), channel_id=1, source_target_pairs={{0,8},{8,0},{16,24},{24,16},{1,9},{9,1},{17,25},{25,17},{2,10},{10... | collective-permute-start | bytes 393224 | tf_op jit(solution)/shard_map/ppermute | solution.py:335
  22.6 1.5 %collective-permute-start.4 = (bf16[4,2,8192]{2,1,0:T(2,128)(2,1)S(1)}, bf16[4,2,8192]{2,1,0:T(2,128)(2,1)S(1)}, u32[]{:S(2)}, u32[]{:S(2)}) collective-permute-start(bf16[4,2,8192]{2,1,0:T(2,128)(2,1)S(1)} %join.1.refs_0_), channel_id=1, source_target_pairs={{0,16},{8,24},{16,0},{24,8},{1,17},{9,25},{17,1},{25,9},{2,18},{10... | collective-permute-start | bytes 393224 | tf_op jit(solution)/shard_map/ppermute | solution.py:335
  24.1 2.0 %collective-permute-done.3.refs_1_ = bf16[4,2,8192]{2,1,0:T(2,128)(2,1)S(1)} collective-permute-done((bf16[4,2,8192]{2,1,0:T(2,128)(2,1)S(1)}, bf16[4,2,8192]{2,1,0:T(2,128)(2,1)S(1)}, u32[]{:S(2)}, u32[]{:S(2)}) %collective-permute-start.3) | collective-permute-done | bytes 131104 | tf_op jit(solution)/shard_map/ppermute | solution.py:335
  26.1 2.4 %collective-permute-start.5 = (bf16[4,2,8192]{2,1,0:T(2,128)(2,1)S(1)}, bf16[4,2,8192]{2,1,0:T(2,128)(2,1)S(1)}, u32[]{:S(2)}, u32[]{:S(2)}) collective-permute-start(bf16[4,2,8192]{2,1,0:T(2,128)(2,1)S(1)} %join.1.refs_0_), channel_id=1, source_target_pairs={{0,24},{8,16},{16,8},{24,0},{1,25},{9,17},{17,9},{25,1},{2,26},{10... | collective-permute-start | bytes 393224 | tf_op jit(solution)/shard_map/ppermute | solution.py:335
  28.5 0.4 collective-permute-done.4.refs_2_
  28.9 3.0 %collective-permute-done.5.refs_3_ = bf16[4,2,8192]{2,1,0:T(2,128)(2,1)S(1)} collective-permute-done((bf16[4,2,8192]{2,1,0:T(2,128)(2,1)S(1)}, bf16[4,2,8192]{2,1,0:T(2,128)(2,1)S(1)}, u32[]{:S(2)}, u32[]{:S(2)}) %collective-permute-start.5) | collective-permute-done | bytes 131104 | tf_op jit(solution)/shard_map/ppermute | solution.py:335
  31.9 0.0 collective-permute-done.7.refs_7_
  31.9 0.0 collective-permute-done.6.refs_6_
  31.9 0.0 collective-permute-done.8.refs_9_
  31.9 4.1 %project.1 = f32[16,2,1344]{2,1,0:T(2,128)} custom-call(bf16[4,2,8192]{2,1,0:T(2,128)(2,1)S(1)} %join.1.refs_0_, bf16[4,2,8192]{2,1,0:T(2,128)(2,1)S(1)} %collective-permute-done.3.refs_1_, bf16[4,2,8192]{2,1,0:T(2,128)(2,1)S(1)} %collective-permute-done.4.refs_2_, bf16[4,2,8192]{2,1,0:T(2,128)(2,1)S(1)} %collective-permute-done.5.refs_3_, ...), custom_call_target="tpu_custom_call" | custom-call | tf_op jit(solution)/shard_map/project/pallas_call | solution.py:272
  36.1 7.0 %all-to-all-start = ((f32[16,2,1344]{2,1,0:T(2,128)}), f32[16,2,1344]{2,1,0:T(2,128)S(1)}, u32[]{:S(2)}, u32[]{:S(2)}) async-start(f32[16,2,1344]{2,1,0:T(2,128)} %project.1), calls=%async_computation | async-start | bytes 360448 | tf_op jit(solution)/shard_map/all_to_all | solution.py:367
  43.1 0.0 copy-done
  43.1 7.8 %all-to-all-done.partial_ref = f32[16,2,1344]{2,1,0:T(2,128)S(1)} async-done(((f32[16,2,1344]{2,1,0:T(2,128)}), f32[16,2,1344]{2,1,0:T(2,128)S(1)}, u32[]{:S(2)}, u32[]{:S(2)}) %all-to-all-start) | async-done | bytes 172064 | tf_op jit(solution)/shard_map/all_to_all | solution.py:367
  50.9 0.8 %normalise.1 = bf16[1,2,5376]{2,1,0:T(2,128)(2,1)} custom-call(f32[16,2,1344]{2,1,0:T(2,128)S(1)} %all-to-all-done.partial_ref, f32[1,5376]{1,0:T(1,128)S(1)} %reshape.7.gain_ref), custom_call_target="tpu_custom_call" | custom-call | tf_op jit(solution)/shard_map/normalise/pallas_call | solution.py:307
  (2 shorter events, 0.0 us)
Async XLA Ops:
  3.5 28.4 %collective-permute-start.8 = (bf16[8,168,1024]{2,1,0:T(8,128)(2,1)S(1)}, bf16[8,168,1024]{2,1,0:T(8,128)(2,1)S(1)}, u32[]{:S(2)}, u32[]{:S(2)}) collective-permute-start(bf16[8,168,1024]{2,1,0:T(8,128)(2,1)S(1)} %get-tuple-element.8.refs_8_), channel_id=1, source_target_pairs={{0,1},{1,0},{2,3},{3,2},{4,5},{5,4},{6,7},{7,6},{8,9},{9,8},{10,11... | collective-permute-start | bytes 8257544 | tf_op jit(solution)/shard_map/ppermute | solution.py:335
  7.5 24.5 %collective-permute-start.6 = (bf16[8,120,1024]{2,1,0:T(8,128)(2,1)S(1)}, bf16[8,120,1024]{2,1,0:T(8,128)(2,1)S(1)}, u32[]{:S(2)}, u32[]{:S(2)}) collective-permute-start(bf16[8,120,1024]{2,1,0:T(8,128)(2,1)S(1)} %local_change.2.refs_4_), channel_id=1, source_target_pairs={{0,1},{1,0},{2,3},{3,2},{4,5},{5,4},{6,7},{7,6},{8,9},{9,8},{10,11... | collective-permute-start | bytes 5898248 | tf_op jit(solution)/shard_map/ppermute | solution.py:335
  9.5 22.4 %collective-permute-start.7 = (bf16[8,48,1024]{2,1,0:T(8,128)(2,1)S(1)}, bf16[8,48,1024]{2,1,0:T(8,128)(2,1)S(1)}, u32[]{:S(2)}, u32[]{:S(2)}) collective-permute-start(bf16[8,48,1024]{2,1,0:T(8,128)(2,1)S(1)} %local_change.3.refs_5_), channel_id=1, source_target_pairs={{0,1},{1,0},{2,3},{3,2},{4,5},{5,4},{6,7},{7,6},{8,9},{9,8},{10,11... | collective-permute-start | bytes 2359304 | tf_op jit(solution)/shard_map/ppermute | solution.py:335
  10.0 5.2 %collective-permute-start = (bf16[1,2,8192]{2,1,0:T(2,128)(2,1)S(1)}, bf16[1,2,8192]{2,1,0:T(2,128)(2,1)S(1)}, u32[]{:S(2)}, u32[]{:S(2)}) collective-permute-start(bf16[1,2,8192]{2,1,0:T(2,128)(2,1)S(1)} %get-tuple-element.7.refs_0_), channel_id=1, source_target_pairs={{0,2},{1,3},{2,0},{3,1},{4,6},{5,7},{6,4},{7,5},{8,10},{9,11},{10,... | collective-permute-start | bytes 98312 | tf_op jit(solution)/shard_map/ppermute | solution.py:335
  12.7 5.9 %collective-permute-start.1 = (bf16[1,2,8192]{2,1,0:T(2,128)(2,1)S(1)}, bf16[1,2,8192]{2,1,0:T(2,128)(2,1)S(1)}, u32[]{:S(2)}, u32[]{:S(2)}) collective-permute-start(bf16[1,2,8192]{2,1,0:T(2,128)(2,1)S(1)} %get-tuple-element.7.refs_0_), channel_id=1, source_target_pairs={{0,4},{1,5},{2,6},{3,7},{4,0},{5,1},{6,2},{7,3},{8,12},{9,13},{10,... | collective-permute-start | bytes 98312 | tf_op jit(solution)/shard_map/ppermute | solution.py:335
  15.3 5.7 %collective-permute-start.2 = (bf16[1,2,8192]{2,1,0:T(2,128)(2,1)S(1)}, bf16[1,2,8192]{2,1,0:T(2,128)(2,1)S(1)}, u32[]{:S(2)}, u32[]{:S(2)}) collective-permute-start(bf16[1,2,8192]{2,1,0:T(2,128)(2,1)S(1)} %get-tuple-element.7.refs_0_), channel_id=1, source_target_pairs={{0,6},{1,7},{2,4},{3,5},{4,2},{5,3},{6,0},{7,1},{8,14},{9,15},{10,... | collective-permute-start | bytes 98312 | tf_op jit(solution)/shard_map/ppermute | solution.py:335
  21.0 22.1 %copy-start = (f32[5376]{0:T(1024)S(1)}, f32[5376]{0:T(1024)}, u32[]{:S(2)}) copy-start(f32[5376]{0:T(1024)} %param.13) | copy-start | bytes 64516
  21.0 5.0 %collective-permute-start.3 = (bf16[4,2,8192]{2,1,0:T(2,128)(2,1)S(1)}, bf16[4,2,8192]{2,1,0:T(2,128)(2,1)S(1)}, u32[]{:S(2)}, u32[]{:S(2)}) collective-permute-start(bf16[4,2,8192]{2,1,0:T(2,128)(2,1)S(1)} %join.1.refs_0_), channel_id=1, source_target_pairs={{0,8},{8,0},{16,24},{24,16},{1,9},{9,1},{17,25},{25,17},{2,10},{10... | collective-permute-start | bytes 393224 | tf_op jit(solution)/shard_map/ppermute | solution.py:335
  22.6 6.4 %collective-permute-start.4 = (bf16[4,2,8192]{2,1,0:T(2,128)(2,1)S(1)}, bf16[4,2,8192]{2,1,0:T(2,128)(2,1)S(1)}, u32[]{:S(2)}, u32[]{:S(2)}) collective-permute-start(bf16[4,2,8192]{2,1,0:T(2,128)(2,1)S(1)} %join.1.refs_0_), channel_id=1, source_target_pairs={{0,16},{8,24},{16,0},{24,8},{1,17},{9,25},{17,1},{25,9},{2,18},{10... | collective-permute-start | bytes 393224 | tf_op jit(solution)/shard_map/ppermute | solution.py:335
  26.1 5.9 %collective-permute-start.5 = (bf16[4,2,8192]{2,1,0:T(2,128)(2,1)S(1)}, bf16[4,2,8192]{2,1,0:T(2,128)(2,1)S(1)}, u32[]{:S(2)}, u32[]{:S(2)}) collective-permute-start(bf16[4,2,8192]{2,1,0:T(2,128)(2,1)S(1)} %join.1.refs_0_), channel_id=1, source_target_pairs={{0,24},{8,16},{16,8},{24,0},{1,25},{9,17},{17,9},{25,1},{2,26},{10... | collective-permute-start | bytes 393224 | tf_op jit(solution)/shard_map/ppermute | solution.py:335
  36.1 14.8 %all-to-all-start = ((f32[16,2,1344]{2,1,0:T(2,128)}), f32[16,2,1344]{2,1,0:T(2,128)S(1)}, u32[]{:S(2)}, u32[]{:S(2)}) async-start(f32[16,2,1344]{2,1,0:T(2,128)} %project.1), calls=%async_computation | async-start | bytes 360448 | tf_op jit(solution)/shard_map/all_to_all | solution.py:367

commit v5 on v4

--- a/solution.py
+++ b/solution.py
@@ -173,43 +173,24 @@
     )(*held(pltpu.VMEM, *parts))
 
 
-def change_kernel(new_hbm, synced_hbm, out_ref, new_ref, synced_ref, sems, *, first, take):
-    blocks, rows, depth = out_ref.shape
-    loads = []
-    for i in range(rows // take):
-        at, near = pl.ds(first + i * take, take), pl.ds(i * take, take)
-        loads.append(
-            (
-                pltpu.make_async_copy(new_hbm.at[at], new_ref.at[near], sems.at[2 * i]),
-                pltpu.make_async_copy(synced_hbm.at[at], synced_ref.at[near], sems.at[2 * i + 1]),
-            )
-        )
-        loads[i][0].start()
-        loads[i][1].start()
-    for i, pair in enumerate(loads):
-        pair[0].wait()
-        pair[1].wait()
-        at = slice(i * take, (i + 1) * take)
-        for b in range(blocks):
-            columns = slice(b * depth, (b + 1) * depth)
-            out_ref[b, at] = (new_ref[at, columns] - synced_ref[at, columns]).astype(jnp.bfloat16)
-
-
-def local_change(new_weight, synced_weight, blocks, first, rows, take):
-    features = new_weight.shape[1]
-    return pl.pallas_call(
-        functools.partial(change_kernel, first=first, take=take),
+def change_kernel(new_ref, synced_ref, out_ref):
+    blocks, _, depth = out_ref.shape
+    for b in range(blocks):
+        columns = slice(b * depth, (b + 1) * depth)
+        out_ref[b] = (new_ref[:, columns] - synced_ref[:, columns]).astype(jnp.bfloat16)
+
+
+def local_change(new_weight, synced_weight, blocks):
+    rows, features = new_weight.shape
+    whole = pl.BlockSpec(memory_space=pltpu.VMEM)
+    return pl.pallas_call(
+        change_kernel,
         out_shape=pltpu.VMEM((blocks, rows, features // blocks), jnp.bfloat16),
-        in_specs=[pl.BlockSpec(memory_space=pltpu.HBM)] * 2,
-        out_specs=pl.BlockSpec(memory_space=pltpu.VMEM),
-        scratch_shapes=[
-            pltpu.VMEM((rows, features), jnp.float32),
-            pltpu.VMEM((rows, features), jnp.float32),
-            pltpu.SemaphoreType.DMA((2 * (rows // take),)),
-        ],
-        compiler_params=limit(14),
+        in_specs=[whole] * 2,
+        out_specs=whole,
+        compiler_params=limit(4),
         name="local_change",
-    )(*held(pltpu.HBM, new_weight, synced_weight))
+    )(*held(pltpu.VMEM, new_weight, synced_weight))
 
 
 def project_kernel(*refs, parts, cuts):
@@ -337,10 +318,7 @@
     def fits(size):
         return size <= FEW and size & (size - 1) == 0
 
-    rows = new_weight.shape[0]
-    take = divisor(rows, 24, 8)
-    early = (rows // take - rows // take // 3) * take
-    stored = resident.reshape(groups * devices, rows, resident.shape[1])
+    stored = resident.reshape(groups * devices, -1, resident.shape[1])
     attended, own_rows = attend(query, cache_keys, cache_values, new_keys, new_values, cache_lengths, stored, devices)
     other_rows = exchange(own_rows, "tensor", devices, 1, 1)
     near = fits(chips) and fits(groups)
@@ -358,12 +336,9 @@
             gathered.append(exchange(column, "dp", groups, 1, hop))
     else:
         gathered = [lax.all_gather(column, "dp", axis=0, tiled=True)]
-    own, swapped = [], []
-    for first, size in ((0, early), (early, rows - early)):
-        if size:
-            own.append(local_change(new_weight, synced_weight, devices, first, size, take))
-            swapped.append(exchange(own[-1], "tensor", devices, 1, 1))
-    partial = project(gathered, own + swapped, own_rows, other_rows, groups * chips * count, steps)
+    own = local_change(new_weight, synced_weight, devices)
+    swapped = exchange(own, "tensor", devices, 1, 1)
+    partial = project(gathered, [own, swapped], own_rows, other_rows, groups * chips * count, steps)
     summed = lax.all_to_all(
         partial,
         ("dp", "tensor"),

time: 52 us -> 44.4 us (0.85)
  starting transfers between devices: 22.3 us -> 13.4 us
  Pallas kernels: 13.1 us -> 8.42 us
  waiting for transfers between devices: 15.5 us -> 19 us
  local copies, waits for them, and re-layouts: 0.02 us -> 2.48 us
    ppermute x9 -> x8, starting transfers between devices: 15.3 us -> 9.9 us  [exchange(): lax.ppermute(value, axis, [(i, (i // unit ^ hop) * unit + i % unit) for i...]
    pallas_call x2 -> x1, Pallas kernels: 5.34 us -> 0.48 us  [local_change(): pl.pallas_call(change_kernel, out_shape=pltpu.VMEM((blocks, rows, feature...]
    ppermute x9 -> x8, waiting for transfers between devices: 7.75 us -> 11.3 us  [exchange(): lax.ppermute(value, axis, [(i, (i // unit ^ hop) * unit + i % unit) for i...]
    all_to_all x1, starting transfers between devices: 6.99 us -> 3.52 us  [body(): lax.all_to_all(partial, ('dp', 'tensor'), split_axis=0, concat_axis=0, ti...]
    unnamed x2 -> x8, local copies, waits for them, and re-layouts: 0.01 us -> 2.46 us
  transfers between devices with their start and end apart: 10 -> 9, of which waited for: 5 -> 5; matrix products, arithmetic and copies ran while one was open for 0% -> 0% of each run, Pallas kernels for 10% -> 1%
where the time goes in v5:
time: 44.4 us; the launch traced here: 44.1 us
  waiting for transfers between devices  19 us (43%)
  starting transfers between devices  13.4 us (30%)
  Pallas kernels  8.42 us (19%)
  local copies, waits for them, and re-layouts  2.48 us (6%)
  between operations  0.74 us (2%)
    ppermute x8, waiting for transfers between devices, exchange(): lax.ppermute(value, axis, [(i, (i // unit ^ hop) * unit + i % unit) for i...  11.3 us
    ppermute x8, starting transfers between devices, exchange(): lax.ppermute(value, axis, [(i, (i // unit ^ hop) * unit + i % unit) for i...  9.9 us
    all_to_all x1, waiting for transfers between devices, body(): lax.all_to_all(partial, ('dp', 'tensor'), split_axis=0, concat_axis=0, ti...  7.75 us
    pallas_call x1, Pallas kernels, project(): pl.pallas_call(functools.partial(project_kernel, parts=len(gathered), cut...  4.13 us
    all_to_all x1, starting transfers between devices, body(): lax.all_to_all(partial, ('dp', 'tensor'), split_axis=0, concat_axis=0, ti...  3.52 us
    pallas_call x1, Pallas kernels, attend(): pl.pallas_call(functools.partial(attend_kernel, width=width), out_shape=[...  2.98 us
    unnamed x8, local copies, waits for them, and re-layouts  2.46 us
  transfers between devices with their start and end apart: 9, of which 5 were waited for; matrix products, arithmetic and copies ran while one was open for 0% of the time, Pallas kernels for 1%

profile of v5, /device:TPU:0, one launch (start us, length us, event | category | flops | bytes accessed | tf_op | source)
XLA Modules:
  0.0 44.1 jit_solution(18298228391578224184)
XLA Ops:
  0.7 0.0 slice-start
  0.7 0.0 slice-start.1
  0.7 0.0 copy-start
  0.7 3.0 %attend.1 = (bf16[1,2,8192]{2,1,0:T(2,128)(2,1)S(1)}, bf16[8,168,1024]{2,1,0:T(8,128)(2,1)S(1)}) custom-call(s32[1]{0:T(128)S(6)} %copy.11.lengths_ref, bf16[1,2,8192]{2,1,0:T(2,128)(2,1)} %query_hbm.1, bf16[1,768,1024]{2,1,0:T(8,128)(2,1)} %keys_hbm.1, bf16[1,768,1024]{2,1,0:T(8,128)(2,1)} %values_hbm.1, bf16[1,2,1024]{2,1,0:T(2,128)(2,1)} %new_keys_hbm.1, ...), custom_call_target="tpu_custom_call" | custom-call | tf_op jit(solution)/shard_map/attend/pallas_call | solution.py:140
  3.7 0.6 %collective-permute-start.7 = (bf16[8,168,1024]{2,1,0:T(8,128)(2,1)S(1)}, bf16[8,168,1024]{2,1,0:T(8,128)(2,1)S(1)}, u32[]{:S(2)}, u32[]{:S(2)}) collective-permute-start(bf16[8,168,1024]{2,1,0:T(8,128)(2,1)S(1)} %get-tuple-element.8.refs_6_), channel_id=1, source_target_pairs={{0,1},{1,0},{2,3},{3,2},{4,5},{5,4},{6,7},{7,6},{8,9},{9,8},{10,11... | collective-permute-start | bytes 8257544 | tf_op jit(solution)/shard_map/ppermute | solution.py:316
  4.2 0.4 slice-done
  4.6 0.4 slice-done.1
  5.0 1.6 %copy-done = f32[168,8192]{1,0:T(8,128)S(1)} copy-done((f32[168,8192]{1,0:T(8,128)S(1)}, f32[168,8192]{1,0:T(8,128)}, u32[]{:S(2)}) %copy-start) | copy-done | bytes 5505048
  6.7 0.5 %local_change.1.refs_4_ = bf16[8,168,1024]{2,1,0:T(8,128)(2,1)S(1)} custom-call(f32[168,8192]{1,0:T(8,128)S(1)} %bitcast.2, f32[168,8192]{1,0:T(8,128)S(1)} %copy-done), custom_call_target="tpu_custom_call" | custom-call | tf_op jit(solution)/shard_map/local_change/pallas_call | solution.py:186
  7.2 0.6 %collective-permute-start.6 = (bf16[8,168,1024]{2,1,0:T(8,128)(2,1)S(1)}, bf16[8,168,1024]{2,1,0:T(8,128)(2,1)S(1)}, u32[]{:S(2)}, u32[]{:S(2)}) collective-permute-start(bf16[8,168,1024]{2,1,0:T(8,128)(2,1)S(1)} %local_change.1.refs_4_), channel_id=1, source_target_pairs={{0,1},{1,0},{2,3},{3,2},{4,5},{5,4},{6,7},{7,6},{8,9},{9,8},{10,11... | collective-permute-start | bytes 8257544 | tf_op jit(solution)/shard_map/ppermute | solution.py:316
  7.7 2.6 %collective-permute-start = (bf16[1,2,8192]{2,1,0:T(2,128)(2,1)S(1)}, bf16[1,2,8192]{2,1,0:T(2,128)(2,1)S(1)}, u32[]{:S(2)}, u32[]{:S(2)}) collective-permute-start(bf16[1,2,8192]{2,1,0:T(2,128)(2,1)S(1)} %get-tuple-element.7.refs_0_), channel_id=1, source_target_pairs={{0,2},{1,3},{2,0},{3,1},{4,6},{5,7},{6,4},{7,5},{8,10},{9,11},{10,... | collective-permute-start | bytes 98312 | tf_op jit(solution)/shard_map/ppermute | solution.py:316
  10.4 2.6 %collective-permute-start.1 = (bf16[1,2,8192]{2,1,0:T(2,128)(2,1)S(1)}, bf16[1,2,8192]{2,1,0:T(2,128)(2,1)S(1)}, u32[]{:S(2)}, u32[]{:S(2)}) collective-permute-start(bf16[1,2,8192]{2,1,0:T(2,128)(2,1)S(1)} %get-tuple-element.7.refs_0_), channel_id=1, source_target_pairs={{0,4},{1,5},{2,6},{3,7},{4,0},{5,1},{6,2},{7,3},{8,12},{9,13},{10,... | collective-permute-start | bytes 98312 | tf_op jit(solution)/shard_map/ppermute | solution.py:316
  12.9 0.0 collective-permute-start.2
  12.9 0.0 collective-permute-done.refs_1_
  12.9 2.8 %collective-permute-done.1.refs_2_ = bf16[1,2,8192]{2,1,0:T(2,128)(2,1)S(1)} collective-permute-done((bf16[1,2,8192]{2,1,0:T(2,128)(2,1)S(1)}, bf16[1,2,8192]{2,1,0:T(2,128)(2,1)S(1)}, u32[]{:S(2)}, u32[]{:S(2)}) %collective-permute-start.1) | collective-permute-done | bytes 32800 | tf_op jit(solution)/shard_map/ppermute | solution.py:316
  15.7 2.9 %collective-permute-done.2.refs_3_ = bf16[1,2,8192]{2,1,0:T(2,128)(2,1)S(1)} collective-permute-done((bf16[1,2,8192]{2,1,0:T(2,128)(2,1)S(1)}, bf16[1,2,8192]{2,1,0:T(2,128)(2,1)S(1)}, u32[]{:S(2)}, u32[]{:S(2)}) %collective-permute-start.2) | collective-permute-done | bytes 32800 | tf_op jit(solution)/shard_map/ppermute | solution.py:316
  18.7 0.0 copy-start.1
  18.7 1.6 %collective-permute-start.3 = (bf16[4,2,8192]{2,1,0:T(2,128)(2,1)S(1)}, bf16[4,2,8192]{2,1,0:T(2,128)(2,1)S(1)}, u32[]{:S(2)}, u32[]{:S(2)}) collective-permute-start(bf16[4,2,8192]{2,1,0:T(2,128)(2,1)S(1)} %join.1.refs_0_), channel_id=1, source_target_pairs={{0,8},{8,0},{16,24},{24,16},{1,9},{9,1},{17,25},{25,17},{2,10},{10... | collective-permute-start | bytes 393224 | tf_op jit(solution)/shard_map/ppermute | solution.py:316
  20.2 1.5 %collective-permute-start.4 = (bf16[4,2,8192]{2,1,0:T(2,128)(2,1)S(1)}, bf16[4,2,8192]{2,1,0:T(2,128)(2,1)S(1)}, u32[]{:S(2)}, u32[]{:S(2)}) collective-permute-start(bf16[4,2,8192]{2,1,0:T(2,128)(2,1)S(1)} %join.1.refs_0_), channel_id=1, source_target_pairs={{0,16},{8,24},{16,0},{24,8},{1,17},{9,25},{17,1},{25,9},{2,18},{10... | collective-permute-start | bytes 393224 | tf_op jit(solution)/shard_map/ppermute | solution.py:316
  21.8 0.5 %collective-permute-start.5 = (bf16[4,2,8192]{2,1,0:T(2,128)(2,1)S(1)}, bf16[4,2,8192]{2,1,0:T(2,128)(2,1)S(1)}, u32[]{:S(2)}, u32[]{:S(2)}) collective-permute-start(bf16[4,2,8192]{2,1,0:T(2,128)(2,1)S(1)} %join.1.refs_0_), channel_id=1, source_target_pairs={{0,24},{8,16},{16,8},{24,0},{1,25},{9,17},{17,9},{25,1},{2,26},{10... | collective-permute-start | bytes 393224 | tf_op jit(solution)/shard_map/ppermute | solution.py:316
  22.2 2.7 %collective-permute-done.3.refs_1_ = bf16[4,2,8192]{2,1,0:T(2,128)(2,1)S(1)} collective-permute-done((bf16[4,2,8192]{2,1,0:T(2,128)(2,1)S(1)}, bf16[4,2,8192]{2,1,0:T(2,128)(2,1)S(1)}, u32[]{:S(2)}, u32[]{:S(2)}) %collective-permute-start.3) | collective-permute-done | bytes 131104 | tf_op jit(solution)/shard_map/ppermute | solution.py:316
  25.0 2.8 %collective-permute-done.4.refs_2_ = bf16[4,2,8192]{2,1,0:T(2,128)(2,1)S(1)} collective-permute-done((bf16[4,2,8192]{2,1,0:T(2,128)(2,1)S(1)}, bf16[4,2,8192]{2,1,0:T(2,128)(2,1)S(1)}, u32[]{:S(2)}, u32[]{:S(2)}) %collective-permute-start.4) | collective-permute-done | bytes 131104 | tf_op jit(solution)/shard_map/ppermute | solution.py:316
  27.8 0.0 collective-permute-done.5.refs_3_
  27.8 0.0 collective-permute-done.7.refs_7_
  27.8 0.0 collective-permute-done.6.refs_5_
  27.8 4.1 %project.1 = f32[16,2,1344]{2,1,0:T(2,128)} custom-call(bf16[4,2,8192]{2,1,0:T(2,128)(2,1)S(1)} %join.1.refs_0_, bf16[4,2,8192]{2,1,0:T(2,128)(2,1)S(1)} %collective-permute-done.3.refs_1_, bf16[4,2,8192]{2,1,0:T(2,128)(2,1)S(1)} %collective-permute-done.4.refs_2_, bf16[4,2,8192]{2,1,0:T(2,128)(2,1)S(1)} %collective-permute-done.5.refs_3_, ...), custom_call_target="tpu_custom_call" | custom-call | tf_op jit(solution)/shard_map/project/pallas_call | solution.py:253
  32.0 3.5 %all-to-all-start = ((f32[16,2,1344]{2,1,0:T(2,128)}), f32[16,2,1344]{2,1,0:T(2,128)S(1)}, u32[]{:S(2)}, u32[]{:S(2)}) async-start(f32[16,2,1344]{2,1,0:T(2,128)} %project.1), calls=%async_computation | async-start | bytes 360448 | tf_op jit(solution)/shard_map/all_to_all | solution.py:342
  35.5 0.0 copy-done.1
  35.5 7.7 %all-to-all-done.partial_ref = f32[16,2,1344]{2,1,0:T(2,128)S(1)} async-done(((f32[16,2,1344]{2,1,0:T(2,128)}), f32[16,2,1344]{2,1,0:T(2,128)S(1)}, u32[]{:S(2)}, u32[]{:S(2)}) %all-to-all-start) | async-done | bytes 172064 | tf_op jit(solution)/shard_map/all_to_all | solution.py:342
  43.3 0.8 %normalise.1 = bf16[1,2,5376]{2,1,0:T(2,128)(2,1)} custom-call(f32[16,2,1344]{2,1,0:T(2,128)S(1)} %all-to-all-done.partial_ref, f32[1,5376]{1,0:T(1,128)S(1)} %reshape.7.gain_ref), custom_call_target="tpu_custom_call" | custom-call | tf_op jit(solution)/shard_map/normalise/pallas_call | solution.py:288
  (3 shorter events, 0.0 us)
Async XLA Ops:
  0.7 4.0 %slice-start = ((s8[5505024]{0:T(1024)(128)(4,1)}), s8[4194304]{0:T(1024)(128)(4,1)S(1)}, s32[]{:S(2)}) async-start(s8[5505024]{0:T(1024)(128)(4,1)} %bitcast.1), calls=%async_computation.1 | async-start | bytes 8388608
  0.7 4.4 %slice-start.1 = ((s8[5505024]{0:T(1024)(128)(4,1)}), s8[1310720]{0:T(1024)(128)(4,1)S(1)}, s32[]{:S(2)}) async-start(s8[5505024]{0:T(1024)(128)(4,1)} %bitcast.1), calls=%async_computation.2 | async-start | bytes 2621440
  0.7 6.0 %copy-start = (f32[168,8192]{1,0:T(8,128)S(1)}, f32[168,8192]{1,0:T(8,128)}, u32[]{:S(2)}) copy-start(f32[168,8192]{1,0:T(8,128)} %synced_ref.1) | copy-start | bytes 16515076
  3.7 24.2 %collective-permute-start.7 = (bf16[8,168,1024]{2,1,0:T(8,128)(2,1)S(1)}, bf16[8,168,1024]{2,1,0:T(8,128)(2,1)S(1)}, u32[]{:S(2)}, u32[]{:S(2)}) collective-permute-start(bf16[8,168,1024]{2,1,0:T(8,128)(2,1)S(1)} %get-tuple-element.8.refs_6_), channel_id=1, source_target_pairs={{0,1},{1,0},{2,3},{3,2},{4,5},{5,4},{6,7},{7,6},{8,9},{9,8},{10,11... | collective-permute-start | bytes 8257544 | tf_op jit(solution)/shard_map/ppermute | solution.py:316
  7.2 20.7 %collective-permute-start.6 = (bf16[8,168,1024]{2,1,0:T(8,128)(2,1)S(1)}, bf16[8,168,1024]{2,1,0:T(8,128)(2,1)S(1)}, u32[]{:S(2)}, u32[]{:S(2)}) collective-permute-start(bf16[8,168,1024]{2,1,0:T(8,128)(2,1)S(1)} %local_change.1.refs_4_), channel_id=1, source_target_pairs={{0,1},{1,0},{2,3},{3,2},{4,5},{5,4},{6,7},{7,6},{8,9},{9,8},{10,11... | collective-permute-start | bytes 8257544 | tf_op jit(solution)/shard_map/ppermute | solution.py:316
  7.7 5.2 %collective-permute-start = (bf16[1,2,8192]{2,1,0:T(2,128)(2,1)S(1)}, bf16[1,2,8192]{2,1,0:T(2,128)(2,1)S(1)}, u32[]{:S(2)}, u32[]{:S(2)}) collective-permute-start(bf16[1,2,8192]{2,1,0:T(2,128)(2,1)S(1)} %get-tuple-element.7.refs_0_), channel_id=1, source_target_pairs={{0,2},{1,3},{2,0},{3,1},{4,6},{5,7},{6,4},{7,5},{8,10},{9,11},{10,... | collective-permute-start | bytes 98312 | tf_op jit(solution)/shard_map/ppermute | solution.py:316
  10.4 5.4 %collective-permute-start.1 = (bf16[1,2,8192]{2,1,0:T(2,128)(2,1)S(1)}, bf16[1,2,8192]{2,1,0:T(2,128)(2,1)S(1)}, u32[]{:S(2)}, u32[]{:S(2)}) collective-permute-start(bf16[1,2,8192]{2,1,0:T(2,128)(2,1)S(1)} %get-tuple-element.7.refs_0_), channel_id=1, source_target_pairs={{0,4},{1,5},{2,6},{3,7},{4,0},{5,1},{6,2},{7,3},{8,12},{9,13},{10,... | collective-permute-start | bytes 98312 | tf_op jit(solution)/shard_map/ppermute | solution.py:316
  12.9 5.7 %collective-permute-start.2 = (bf16[1,2,8192]{2,1,0:T(2,128)(2,1)S(1)}, bf16[1,2,8192]{2,1,0:T(2,128)(2,1)S(1)}, u32[]{:S(2)}, u32[]{:S(2)}) collective-permute-start(bf16[1,2,8192]{2,1,0:T(2,128)(2,1)S(1)} %get-tuple-element.7.refs_0_), channel_id=1, source_target_pairs={{0,6},{1,7},{2,4},{3,5},{4,2},{5,3},{6,0},{7,1},{8,14},{9,15},{10,... | collective-permute-start | bytes 98312 | tf_op jit(solution)/shard_map/ppermute | solution.py:316
  18.7 16.8 %copy-start.1 = (f32[5376]{0:T(1024)S(1)}, f32[5376]{0:T(1024)}, u32[]{:S(2)}) copy-start(f32[5376]{0:T(1024)} %param.13) | copy-start | bytes 64516
  18.7 6.3 %collective-permute-start.3 = (bf16[4,2,8192]{2,1,0:T(2,128)(2,1)S(1)}, bf16[4,2,8192]{2,1,0:T(2,128)(2,1)S(1)}, u32[]{:S(2)}, u32[]{:S(2)}) collective-permute-start(bf16[4,2,8192]{2,1,0:T(2,128)(2,1)S(1)} %join.1.refs_0_), channel_id=1, source_target_pairs={{0,8},{8,0},{16,24},{24,16},{1,9},{9,1},{17,25},{25,17},{2,10},{10... | collective-permute-start | bytes 393224 | tf_op jit(solution)/shard_map/ppermute | solution.py:316
  20.2 7.6 %collective-permute-start.4 = (bf16[4,2,8192]{2,1,0:T(2,128)(2,1)S(1)}, bf16[4,2,8192]{2,1,0:T(2,128)(2,1)S(1)}, u32[]{:S(2)}, u32[]{:S(2)}) collective-permute-start(bf16[4,2,8192]{2,1,0:T(2,128)(2,1)S(1)} %join.1.refs_0_), channel_id=1, source_target_pairs={{0,16},{8,24},{16,0},{24,8},{1,17},{9,25},{17,1},{25,9},{2,18},{10... | collective-permute-start | bytes 393224 | tf_op jit(solution)/shard_map/ppermute | solution.py:316
  21.8 6.1 %collective-permute-start.5 = (bf16[4,2,8192]{2,1,0:T(2,128)(2,1)S(1)}, bf16[4,2,8192]{2,1,0:T(2,128)(2,1)S(1)}, u32[]{:S(2)}, u32[]{:S(2)}) collective-permute-start(bf16[4,2,8192]{2,1,0:T(2,128)(2,1)S(1)} %join.1.refs_0_), channel_id=1, source_target_pairs={{0,24},{8,16},{16,8},{24,0},{1,25},{9,17},{17,9},{25,1},{2,26},{10... | collective-permute-start | bytes 393224 | tf_op jit(solution)/shard_map/ppermute | solution.py:316
  32.0 11.3 %all-to-all-start = ((f32[16,2,1344]{2,1,0:T(2,128)}), f32[16,2,1344]{2,1,0:T(2,128)S(1)}, u32[]{:S(2)}, u32[]{:S(2)}) async-start(f32[16,2,1344]{2,1,0:T(2,128)} %project.1), calls=%async_computation | async-start | bytes 360448 | tf_op jit(solution)/shard_map/all_to_all | solution.py:342

commit v6 on v5

--- a/solution.py
+++ b/solution.py
@@ -76,7 +76,7 @@
         for load in loads:
             load.start()
         if row == 0:
-            near.start()
+            near.start(priority=1)
 
         padding = jnp.zeros((8 - steps % 8, kv_features), jnp.float32)
         loads[0].wait()
@@ -155,17 +155,16 @@
 
 def join_kernel(*refs):
     *part_refs, out_ref = refs
-    count = part_refs[0].shape[0]
-    for i, ref in enumerate(part_refs):
-        out_ref[i * count : (i + 1) * count] = ref[...]
+    rows = [ref[k].astype(jnp.float32) for ref in part_refs for k in range(ref.shape[0])]
+    out_ref[...] = jnp.concatenate(rows, axis=0).astype(out_ref.dtype)
 
 
 def join(parts):
     whole = pl.BlockSpec(memory_space=pltpu.VMEM)
-    count = parts[0].shape[0]
+    count, steps, features = parts[0].shape
     return pl.pallas_call(
         join_kernel,
-        out_shape=pltpu.VMEM((count * len(parts), *parts[0].shape[1:]), parts[0].dtype),
+        out_shape=pltpu.VMEM((len(parts) * count * steps, features), parts[0].dtype),
         in_specs=[whole] * len(parts),
         out_specs=whole,
         compiler_params=limit(4),
@@ -202,11 +201,13 @@
     places = (device, device ^ 1)
     group, chip = lax.axis_index("dp"), device // CORES
 
-    pieces = []
-    for part in gathered:
-        for k in range(part.shape[0]):
-            pieces.append(part[k].astype(jnp.float32))
-    rows_ref[...] = jnp.concatenate(pieces, axis=0).astype(jnp.bfloat16)
+    for i, part in enumerate(gathered):
+        if parts > 1:
+            value = part[...]
+        else:
+            pieces = [part[k].astype(jnp.float32) for k in range(owners)]
+            value = jnp.concatenate(pieces, axis=0).astype(jnp.bfloat16)
+        rows_ref[i * len(value) : (i + 1) * len(value)] = value
 
     deltas = []
     for ref in changes:

time: 44.4 us -> 44.4 us (level)
  no operation moved by 1% of the time
where the time goes in v6:
time: 44.4 us; the launch traced here: 44.2 us
  waiting for transfers between devices  19 us (43%)
  starting transfers between devices  13.4 us (30%)
  Pallas kernels  8.46 us (19%)
  local copies, waits for them, and re-layouts  2.51 us (6%)
  between operations  0.74 us (2%)
    ppermute x8, waiting for transfers between devices, exchange(): lax.ppermute(value, axis, [(i, (i // unit ^ hop) * unit + i % unit) for i...  11.3 us
    ppermute x8, starting transfers between devices, exchange(): lax.ppermute(value, axis, [(i, (i // unit ^ hop) * unit + i % unit) for i...  9.9 us
    all_to_all x1, waiting for transfers between devices, body(): lax.all_to_all(partial, ('dp', 'tensor'), split_axis=0, concat_axis=0, ti...  7.75 us
    pallas_call x1, Pallas kernels, project(): pl.pallas_call(functools.partial(project_kernel, parts=len(gathered), cut...  4.09 us
    all_to_all x1, starting transfers between devices, body(): lax.all_to_all(partial, ('dp', 'tensor'), split_axis=0, concat_axis=0, ti...  3.52 us
    pallas_call x1, Pallas kernels, attend(): pl.pallas_call(functools.partial(attend_kernel, width=width), out_shape=[...  2.97 us
    unnamed x8, local copies, waits for them, and re-layouts  2.49 us
  transfers between devices with their start and end apart: 9, of which 5 were waited for; matrix products, arithmetic and copies ran while one was open for 0% of the time, Pallas kernels for 1%

profile of v6, /device:TPU:0, one launch (start us, length us, event | category | flops | bytes accessed | tf_op | source)
XLA Modules:
  0.0 44.2 jit_solution(14870938783466979280)
XLA Ops:
  0.7 0.0 slice-start
  0.7 0.0 slice-start.1
  0.7 0.0 copy-start
  0.7 3.0 %attend.1 = (bf16[1,2,8192]{2,1,0:T(2,128)(2,1)S(1)}, bf16[8,168,1024]{2,1,0:T(8,128)(2,1)S(1)}) custom-call(s32[1]{0:T(128)S(6)} %copy.11.lengths_ref, bf16[1,2,8192]{2,1,0:T(2,128)(2,1)} %query_hbm.1, bf16[1,768,1024]{2,1,0:T(8,128)(2,1)} %keys_hbm.1, bf16[1,768,1024]{2,1,0:T(8,128)(2,1)} %values_hbm.1, bf16[1,2,1024]{2,1,0:T(2,128)(2,1)} %new_keys_hbm.1, ...), custom_call_target="tpu_custom_call" | custom-call | tf_op jit(solution)/shard_map/attend/pallas_call | solution.py:140
  3.7 0.6 %collective-permute-start.7 = (bf16[8,168,1024]{2,1,0:T(8,128)(2,1)S(1)}, bf16[8,168,1024]{2,1,0:T(8,128)(2,1)S(1)}, u32[]{:S(2)}, u32[]{:S(2)}) collective-permute-start(bf16[8,168,1024]{2,1,0:T(8,128)(2,1)S(1)} %get-tuple-element.8.refs_6_), channel_id=1, source_target_pairs={{0,1},{1,0},{2,3},{3,2},{4,5},{5,4},{6,7},{7,6},{8,9},{9,8},{10,11... | collective-permute-start | bytes 8257544 | tf_op jit(solution)/shard_map/ppermute | solution.py:317
  4.2 0.4 slice-done
  4.7 0.4 slice-done.1
  5.1 1.6 %copy-done = f32[168,8192]{1,0:T(8,128)S(1)} copy-done((f32[168,8192]{1,0:T(8,128)S(1)}, f32[168,8192]{1,0:T(8,128)}, u32[]{:S(2)}) %copy-start) | copy-done | bytes 5505048
  6.7 0.5 %local_change.1.refs_4_ = bf16[8,168,1024]{2,1,0:T(8,128)(2,1)S(1)} custom-call(f32[168,8192]{1,0:T(8,128)S(1)} %bitcast.2, f32[168,8192]{1,0:T(8,128)S(1)} %copy-done), custom_call_target="tpu_custom_call" | custom-call | tf_op jit(solution)/shard_map/local_change/pallas_call | solution.py:185
  7.2 0.6 %collective-permute-start.6 = (bf16[8,168,1024]{2,1,0:T(8,128)(2,1)S(1)}, bf16[8,168,1024]{2,1,0:T(8,128)(2,1)S(1)}, u32[]{:S(2)}, u32[]{:S(2)}) collective-permute-start(bf16[8,168,1024]{2,1,0:T(8,128)(2,1)S(1)} %local_change.1.refs_4_), channel_id=1, source_target_pairs={{0,1},{1,0},{2,3},{3,2},{4,5},{5,4},{6,7},{7,6},{8,9},{9,8},{10,11... | collective-permute-start | bytes 8257544 | tf_op jit(solution)/shard_map/ppermute | solution.py:317
  7.7 2.6 %collective-permute-start = (bf16[1,2,8192]{2,1,0:T(2,128)(2,1)S(1)}, bf16[1,2,8192]{2,1,0:T(2,128)(2,1)S(1)}, u32[]{:S(2)}, u32[]{:S(2)}) collective-permute-start(bf16[1,2,8192]{2,1,0:T(2,128)(2,1)S(1)} %get-tuple-element.7.refs_0_), channel_id=1, source_target_pairs={{0,2},{1,3},{2,0},{3,1},{4,6},{5,7},{6,4},{7,5},{8,10},{9,11},{10,... | collective-permute-start | bytes 98312 | tf_op jit(solution)/shard_map/ppermute | solution.py:317
  10.4 2.6 %collective-permute-start.1 = (bf16[1,2,8192]{2,1,0:T(2,128)(2,1)S(1)}, bf16[1,2,8192]{2,1,0:T(2,128)(2,1)S(1)}, u32[]{:S(2)}, u32[]{:S(2)}) collective-permute-start(bf16[1,2,8192]{2,1,0:T(2,128)(2,1)S(1)} %get-tuple-element.7.refs_0_), channel_id=1, source_target_pairs={{0,4},{1,5},{2,6},{3,7},{4,0},{5,1},{6,2},{7,3},{8,12},{9,13},{10,... | collective-permute-start | bytes 98312 | tf_op jit(solution)/shard_map/ppermute | solution.py:317
  13.0 0.0 collective-permute-start.2
  13.0 0.0 collective-permute-done.refs_1_
  13.0 2.8 %collective-permute-done.1.refs_2_ = bf16[1,2,8192]{2,1,0:T(2,128)(2,1)S(1)} collective-permute-done((bf16[1,2,8192]{2,1,0:T(2,128)(2,1)S(1)}, bf16[1,2,8192]{2,1,0:T(2,128)(2,1)S(1)}, u32[]{:S(2)}, u32[]{:S(2)}) %collective-permute-start.1) | collective-permute-done | bytes 32800 | tf_op jit(solution)/shard_map/ppermute | solution.py:317
  15.8 2.9 %collective-permute-done.2.refs_3_ = bf16[1,2,8192]{2,1,0:T(2,128)(2,1)S(1)} collective-permute-done((bf16[1,2,8192]{2,1,0:T(2,128)(2,1)S(1)}, bf16[1,2,8192]{2,1,0:T(2,128)(2,1)S(1)}, u32[]{:S(2)}, u32[]{:S(2)}) %collective-permute-start.2) | collective-permute-done | bytes 32800 | tf_op jit(solution)/shard_map/ppermute | solution.py:317
  18.7 0.1 join.1.refs_0_
  18.8 0.0 copy-start.1
  18.8 1.6 %collective-permute-start.3 = (bf16[8,8192]{1,0:T(8,128)(2,1)S(1)}, bf16[8,8192]{1,0:T(8,128)(2,1)S(1)}, u32[]{:S(2)}, u32[]{:S(2)}) collective-permute-start(bf16[8,8192]{1,0:T(8,128)(2,1)S(1)} %join.1.refs_0_), channel_id=1, source_target_pairs={{0,8},{8,0},{16,24},{24,16},{1,9},{9,1},{17,25},{25,17},{2,10},{10... | collective-permute-start | bytes 393224 | tf_op jit(solution)/shard_map/ppermute | solution.py:317
  20.3 1.5 %collective-permute-start.4 = (bf16[8,8192]{1,0:T(8,128)(2,1)S(1)}, bf16[8,8192]{1,0:T(8,128)(2,1)S(1)}, u32[]{:S(2)}, u32[]{:S(2)}) collective-permute-start(bf16[8,8192]{1,0:T(8,128)(2,1)S(1)} %join.1.refs_0_), channel_id=1, source_target_pairs={{0,16},{8,24},{16,0},{24,8},{1,17},{9,25},{17,1},{25,9},{2,18},{10... | collective-permute-start | bytes 393224 | tf_op jit(solution)/shard_map/ppermute | solution.py:317
  21.9 0.5 %collective-permute-start.5 = (bf16[8,8192]{1,0:T(8,128)(2,1)S(1)}, bf16[8,8192]{1,0:T(8,128)(2,1)S(1)}, u32[]{:S(2)}, u32[]{:S(2)}) collective-permute-start(bf16[8,8192]{1,0:T(8,128)(2,1)S(1)} %join.1.refs_0_), channel_id=1, source_target_pairs={{0,24},{8,16},{16,8},{24,0},{1,25},{9,17},{17,9},{25,1},{2,26},{10... | collective-permute-start | bytes 393224 | tf_op jit(solution)/shard_map/ppermute | solution.py:317
  22.3 2.7 %collective-permute-done.3.refs_1_ = bf16[8,8192]{1,0:T(8,128)(2,1)S(1)} collective-permute-done((bf16[8,8192]{1,0:T(8,128)(2,1)S(1)}, bf16[8,8192]{1,0:T(8,128)(2,1)S(1)}, u32[]{:S(2)}, u32[]{:S(2)}) %collective-permute-start.3) | collective-permute-done | bytes 131104 | tf_op jit(solution)/shard_map/ppermute | solution.py:317
  25.1 2.8 %collective-permute-done.4.refs_2_ = bf16[8,8192]{1,0:T(8,128)(2,1)S(1)} collective-permute-done((bf16[8,8192]{1,0:T(8,128)(2,1)S(1)}, bf16[8,8192]{1,0:T(8,128)(2,1)S(1)}, u32[]{:S(2)}, u32[]{:S(2)}) %collective-permute-start.4) | collective-permute-done | bytes 131104 | tf_op jit(solution)/shard_map/ppermute | solution.py:317
  27.9 0.0 collective-permute-done.5.refs_3_
  27.9 0.0 collective-permute-done.7.refs_7_
  27.9 0.0 collective-permute-done.6.refs_5_
  27.9 4.1 %project.1 = f32[16,2,1344]{2,1,0:T(2,128)} custom-call(bf16[8,8192]{1,0:T(8,128)(2,1)S(1)} %join.1.refs_0_, bf16[8,8192]{1,0:T(8,128)(2,1)S(1)} %collective-permute-done.3.refs_1_, bf16[8,8192]{1,0:T(8,128)(2,1)S(1)} %collective-permute-done.4.refs_2_, bf16[8,8192]{1,0:T(8,128)(2,1)S(1)} %collective-permute-done.5.refs_3_, ...), custom_call_target="tpu_custom_call" | custom-call | tf_op jit(solution)/shard_map/project/pallas_call | solution.py:254
  32.0 3.5 %all-to-all-start = ((f32[16,2,1344]{2,1,0:T(2,128)}), f32[16,2,1344]{2,1,0:T(2,128)S(1)}, u32[]{:S(2)}, u32[]{:S(2)}) async-start(f32[16,2,1344]{2,1,0:T(2,128)} %project.1), calls=%async_computation | async-start | bytes 360448 | tf_op jit(solution)/shard_map/all_to_all | solution.py:343
  35.6 0.0 copy-done.1
  35.6 7.7 %all-to-all-done.partial_ref = f32[16,2,1344]{2,1,0:T(2,128)S(1)} async-done(((f32[16,2,1344]{2,1,0:T(2,128)}), f32[16,2,1344]{2,1,0:T(2,128)S(1)}, u32[]{:S(2)}, u32[]{:S(2)}) %all-to-all-start) | async-done | bytes 172064 | tf_op jit(solution)/shard_map/all_to_all | solution.py:343
  43.3 0.8 %normalise.1 = bf16[1,2,5376]{2,1,0:T(2,128)(2,1)} custom-call(f32[16,2,1344]{2,1,0:T(2,128)S(1)} %all-to-all-done.partial_ref, f32[1,5376]{1,0:T(1,128)S(1)} %reshape.7.gain_ref), custom_call_target="tpu_custom_call" | custom-call | tf_op jit(solution)/shard_map/normalise/pallas_call | solution.py:289
  (2 shorter events, 0.0 us)
Async XLA Ops:
  0.7 4.0 %slice-start = ((s8[5505024]{0:T(1024)(128)(4,1)}), s8[4194304]{0:T(1024)(128)(4,1)S(1)}, s32[]{:S(2)}) async-start(s8[5505024]{0:T(1024)(128)(4,1)} %bitcast.1), calls=%async_computation.1 | async-start | bytes 8388608
  0.7 4.4 %slice-start.1 = ((s8[5505024]{0:T(1024)(128)(4,1)}), s8[1310720]{0:T(1024)(128)(4,1)S(1)}, s32[]{:S(2)}) async-start(s8[5505024]{0:T(1024)(128)(4,1)} %bitcast.1), calls=%async_computation.2 | async-start | bytes 2621440
  0.7 6.0 %copy-start = (f32[168,8192]{1,0:T(8,128)S(1)}, f32[168,8192]{1,0:T(8,128)}, u32[]{:S(2)}) copy-start(f32[168,8192]{1,0:T(8,128)} %synced_ref.1) | copy-start | bytes 16515076
  3.7 24.3 %collective-permute-start.7 = (bf16[8,168,1024]{2,1,0:T(8,128)(2,1)S(1)}, bf16[8,168,1024]{2,1,0:T(8,128)(2,1)S(1)}, u32[]{:S(2)}, u32[]{:S(2)}) collective-permute-start(bf16[8,168,1024]{2,1,0:T(8,128)(2,1)S(1)} %get-tuple-element.8.refs_6_), channel_id=1, source_target_pairs={{0,1},{1,0},{2,3},{3,2},{4,5},{5,4},{6,7},{7,6},{8,9},{9,8},{10,11... | collective-permute-start | bytes 8257544 | tf_op jit(solution)/shard_map/ppermute | solution.py:317
  7.2 20.7 %collective-permute-start.6 = (bf16[8,168,1024]{2,1,0:T(8,128)(2,1)S(1)}, bf16[8,168,1024]{2,1,0:T(8,128)(2,1)S(1)}, u32[]{:S(2)}, u32[]{:S(2)}) collective-permute-start(bf16[8,168,1024]{2,1,0:T(8,128)(2,1)S(1)} %local_change.1.refs_4_), channel_id=1, source_target_pairs={{0,1},{1,0},{2,3},{3,2},{4,5},{5,4},{6,7},{7,6},{8,9},{9,8},{10,11... | collective-permute-start | bytes 8257544 | tf_op jit(solution)/shard_map/ppermute | solution.py:317
  7.7 5.2 %collective-permute-start = (bf16[1,2,8192]{2,1,0:T(2,128)(2,1)S(1)}, bf16[1,2,8192]{2,1,0:T(2,128)(2,1)S(1)}, u32[]{:S(2)}, u32[]{:S(2)}) collective-permute-start(bf16[1,2,8192]{2,1,0:T(2,128)(2,1)S(1)} %get-tuple-element.7.refs_0_), channel_id=1, source_target_pairs={{0,2},{1,3},{2,0},{3,1},{4,6},{5,7},{6,4},{7,5},{8,10},{9,11},{10,... | collective-permute-start | bytes 98312 | tf_op jit(solution)/shard_map/ppermute | solution.py:317
  10.4 5.4 %collective-permute-start.1 = (bf16[1,2,8192]{2,1,0:T(2,128)(2,1)S(1)}, bf16[1,2,8192]{2,1,0:T(2,128)(2,1)S(1)}, u32[]{:S(2)}, u32[]{:S(2)}) collective-permute-start(bf16[1,2,8192]{2,1,0:T(2,128)(2,1)S(1)} %get-tuple-element.7.refs_0_), channel_id=1, source_target_pairs={{0,4},{1,5},{2,6},{3,7},{4,0},{5,1},{6,2},{7,3},{8,12},{9,13},{10,... | collective-permute-start | bytes 98312 | tf_op jit(solution)/shard_map/ppermute | solution.py:317
  13.0 5.7 %collective-permute-start.2 = (bf16[1,2,8192]{2,1,0:T(2,128)(2,1)S(1)}, bf16[1,2,8192]{2,1,0:T(2,128)(2,1)S(1)}, u32[]{:S(2)}, u32[]{:S(2)}) collective-permute-start(bf16[1,2,8192]{2,1,0:T(2,128)(2,1)S(1)} %get-tuple-element.7.refs_0_), channel_id=1, source_target_pairs={{0,6},{1,7},{2,4},{3,5},{4,2},{5,3},{6,0},{7,1},{8,14},{9,15},{10,... | collective-permute-start | bytes 98312 | tf_op jit(solution)/shard_map/ppermute | solution.py:317
  18.8 16.8 %copy-start.1 = (f32[5376]{0:T(1024)S(1)}, f32[5376]{0:T(1024)}, u32[]{:S(2)}) copy-start(f32[5376]{0:T(1024)} %param.13) | copy-start | bytes 64516
  18.8 6.3 %collective-permute-start.3 = (bf16[8,8192]{1,0:T(8,128)(2,1)S(1)}, bf16[8,8192]{1,0:T(8,128)(2,1)S(1)}, u32[]{:S(2)}, u32[]{:S(2)}) collective-permute-start(bf16[8,8192]{1,0:T(8,128)(2,1)S(1)} %join.1.refs_0_), channel_id=1, source_target_pairs={{0,8},{8,0},{16,24},{24,16},{1,9},{9,1},{17,25},{25,17},{2,10},{10... | collective-permute-start | bytes 393224 | tf_op jit(solution)/shard_map/ppermute | solution.py:317
  20.3 7.6 %collective-permute-start.4 = (bf16[8,8192]{1,0:T(8,128)(2,1)S(1)}, bf16[8,8192]{1,0:T(8,128)(2,1)S(1)}, u32[]{:S(2)}, u32[]{:S(2)}) collective-permute-start(bf16[8,8192]{1,0:T(8,128)(2,1)S(1)} %join.1.refs_0_), channel_id=1, source_target_pairs={{0,16},{8,24},{16,0},{24,8},{1,17},{9,25},{17,1},{25,9},{2,18},{10... | collective-permute-start | bytes 393224 | tf_op jit(solution)/shard_map/ppermute | solution.py:317
  21.9 6.1 %collective-permute-start.5 = (bf16[8,8192]{1,0:T(8,128)(2,1)S(1)}, bf16[8,8192]{1,0:T(8,128)(2,1)S(1)}, u32[]{:S(2)}, u32[]{:S(2)}) collective-permute-start(bf16[8,8192]{1,0:T(8,128)(2,1)S(1)} %join.1.refs_0_), channel_id=1, source_target_pairs={{0,24},{8,16},{16,8},{24,0},{1,25},{9,17},{17,9},{25,1},{2,26},{10... | collective-permute-start | bytes 393224 | tf_op jit(solution)/shard_map/ppermute | solution.py:317
  32.0 11.3 %all-to-all-start = ((f32[16,2,1344]{2,1,0:T(2,128)}), f32[16,2,1344]{2,1,0:T(2,128)S(1)}, u32[]{:S(2)}, u32[]{:S(2)}) async-start(f32[16,2,1344]{2,1,0:T(2,128)} %project.1), calls=%async_computation | async-start | bytes 360448 | tf_op jit(solution)/shard_map/all_to_all | solution.py:343
